TPU v7x, 256 devices: a whole 4x4x8 slice. The times are simulated.
256 devices in a mesh: dp: 32 (over x, y, core), expert: 8 (over z).
Axes of the slice: x: 4, y: 4, z: 8, core: 2. Of those that a mesh axis runs over, the one named last changes fastest.
Arguments:
- tokens: bfloat16 [1024, 4096], P('expert', 'dp'), may hold values from -6 to 6
- in_signs: int32 [1024, 128], P('expert', 'dp'), may hold values from -2147483648 to 2147483646
- out_signs: int32 [1024, 224], P('expert'), may hold values from -2147483648 to 2147483646
- expert_ids: int32 [1024, 2], P('expert'), may hold values from 0 to 7, all different within a row; in each aligned block of 128 rows (0 to 127, 128 to 255, ...) at most 40 rows name the same one
- route_weight: float32 [1024, 2], P('expert'), may hold values from 0.2 to 1
- cotangent: bfloat16 [1024, 7168], P('expert', 'dp'), may hold values from -6 to 6
- mean_weight: bfloat16 [8, 4096, 7168], P('expert', 'dp'), may hold values from -0.09375 to 0.09375
- rho_weight: bfloat16 [8, 4096, 7168], P('expert', 'dp'), may hold values from -6 to -3
- noise_weight: bfloat16 [8, 4096, 7168], P('expert', 'dp'), may hold values from -4 to 4
Outputs:
- hidden_out: bfloat16 [1024, 7168], P('expert', 'dp')
- grad_tokens: bfloat16 [1024, 4096], P('expert', 'dp')
- grad_mean: bfloat16 [8, 4096, 7168], P('expert', 'dp')
- grad_rho: bfloat16 [8, 4096, 7168], P('expert', 'dp')
Inputs may be any that keep to these rules, and one draw needn't show every extreme that they name: `expert_ids`: each token names 2 different experts. In each aligned block of 128 tokens no expert is named by more than 40 tokens, and in some blocks one expert is named by exactly 40. `in_signs`: bit b of word w, counted from the lowest, is set where the sign of feature 32 * w + b is -1 and clear where it is +1. `out_signs`: bit b of word w, counted from the lowest, is set where the sign of hidden unit 32 * w + b is -1 and clear where it is +1.
All inputs are finite; a program needn't handle non-finite values.
Results may differ from a plain program's by a relative error of at most 0.0071.
Values may be sent and summed in bfloat16 or wider, within the bound.
A program may use at most 128 MiB of HBM per device.

v0:
```python
import jax
import jax.numpy as jnp
from jax import lax
from jax.sharding import PartitionSpec as P


def in_one_piece(arrays, axis, dim, along):
    ends, at = ([], 0)
    for a in arrays[:-1]:
        at += a.shape[along]
        ends.append(at)
    both = jnp.concatenate(arrays, axis=along)
    return tuple(jnp.split(lax.all_gather(both, axis, axis=dim, tiled=True), ends, axis=along))


def unpack_rows(words):
    shifts = jnp.arange(32, dtype=jnp.int32)
    bits = jnp.bitwise_and(jnp.right_shift(words[..., None], shifts), 1)
    signs = (1 - 2 * bits).astype(jnp.float32)
    return signs.reshape(words.shape[:-1] + (words.shape[-1] * 32,))


def unpack_cols(words):
    shifts = jnp.arange(32, dtype=jnp.int32)
    bits = jnp.bitwise_and(jnp.right_shift(words.T[:, None, :], shifts[None, :, None]), 1)
    signs = (1 - 2 * bits).astype(jnp.float32)
    return signs.reshape(words.shape[1] * 32, words.shape[0])


def block_slots(block_ids, experts, capacity):
    onehot = (block_ids[:, :, None] == jnp.arange(experts, dtype=jnp.int32)).astype(jnp.int32)
    flat = onehot.reshape(-1, experts)
    before = jnp.cumsum(flat, axis=0) - flat
    ranks = jnp.sum(before * flat, axis=1).reshape(block_ids.shape)
    return block_ids * capacity + ranks


def on_device(
    tokens,
    in_signs,
    out_signs,
    expert_ids,
    route_weight,
    cotangent,
    mean_weight,
    rho_weight,
    noise_weight,
):
    experts = lax.axis_size("expert") * mean_weight.shape[0]
    token_count = tokens.shape[0]
    topk = expert_ids.shape[1]
    capacity = 5 * token_count * topk // (4 * experts)
    slots = experts * capacity
    width_local = tokens.shape[1]
    sign_words = in_signs.shape[1]
    hidden_local = cotangent.shape[1]
    data_index = lax.axis_index("dp")
    slot_of = block_slots(expert_ids, experts, capacity)
    match = (slot_of[:, :, None] == jnp.arange(slots, dtype=jnp.int32)).astype(jnp.int32)
    token_rank = jnp.arange(token_count, dtype=jnp.int32)[:, None, None]
    slot_token = jnp.sum(match * token_rank, axis=(0, 1))
    slot_fill = jnp.sum(match, axis=(0, 1))
    slot_weight = jnp.sum(match.astype(jnp.float32) * route_weight[:, :, None], axis=(0, 1))
    per_slice = max(1, hidden_local // 32)
    first_unit = data_index * hidden_local
    carried = lax.dynamic_slice_in_dim(out_signs, first_unit // 32, per_slice, 1)
    words = jnp.concatenate([in_signs, carried], axis=1)
    fill_rows = slot_fill.astype(jnp.bfloat16)[:, None]
    send_rows = (jnp.take(tokens, slot_token, axis=0) * fill_rows).reshape(
        experts, capacity, width_local
    )
    send_words = jnp.take(words, slot_token, axis=0).reshape(experts, capacity, words.shape[1])
    recv_rows, recv_words = (
        lax.all_to_all(send_rows, "expert", split_axis=0, concat_axis=0, tiled=True),
        lax.all_to_all(send_words, "expert", split_axis=0, concat_axis=0, tiled=True),
    )
    rows = recv_rows.reshape(slots, width_local)
    recv_words = recv_words.reshape(slots, words.shape[1])
    input_signs = unpack_rows(recv_words[:, :sign_words])
    input_cols = unpack_cols(recv_words[:, :sign_words])
    signed = rows * input_signs.astype(jnp.bfloat16)
    mean_local = mean_weight[0]
    rho_float = rho_weight[0].astype(jnp.float32)
    noise_float = noise_weight[0].astype(jnp.float32)
    delta = (jax.nn.softplus(rho_float) * noise_float).astype(jnp.bfloat16)
    contract = (((0,), (1,)), ((), ()))
    word_signs = unpack_cols(recv_words[:, sign_words:])
    mean_cols = mean_local
    delta_cols = delta
    mean_part = lax.dot_general(mean_cols, rows, contract, preferred_element_type=jnp.float32)
    pert_part = lax.dot_general(delta_cols, signed, contract, preferred_element_type=jnp.float32)
    mean_part, pert_part = (mean_part, pert_part)
    both = lax.psum_scatter(
        jnp.concatenate([mean_part, pert_part], axis=1), "dp", scatter_dimension=0, tiled=True
    )
    preact = both[:, :slots] + word_signs * both[:, slots:]
    gate = jax.nn.sigmoid(preact)
    hidden_slots = (preact * gate).astype(jnp.bfloat16)
    slope = gate * (1.0 + preact * (1.0 - gate))
    returned = lax.all_to_all(
        hidden_slots.reshape(hidden_local, experts, capacity),
        "expert",
        split_axis=1,
        concat_axis=1,
        tiled=True,
    )
    returned = returned.reshape(hidden_local, slots)
    picked = jnp.take(returned, slot_of, axis=1).astype(jnp.float32)
    hidden_out = jnp.sum(picked * route_weight[None], axis=2).T.astype(jnp.bfloat16)
    upstream = jnp.take(cotangent.T, slot_token, axis=1).astype(jnp.float32) * slot_weight[None, :]
    upstream = upstream.astype(jnp.bfloat16).reshape(hidden_local, experts, capacity)
    arrived = lax.all_to_all(upstream, "expert", split_axis=1, concat_axis=1, tiled=True).reshape(
        hidden_local, slots
    )
    grad_preact = (arrived.astype(jnp.float32) * slope).astype(jnp.bfloat16)
    grad_signed_pre = grad_preact * word_signs.astype(jnp.bfloat16)
    pieces = in_one_piece((grad_preact, grad_signed_pre), "dp", 0, 1)
    piece_plain = pieces[0]
    piece_signed = pieces[1]
    mean_cols = mean_local
    delta_cols = delta
    grad_rows = jnp.dot(mean_cols, piece_plain, preferred_element_type=jnp.float32)
    grad_signed = jnp.dot(delta_cols, piece_signed, preferred_element_type=jnp.float32)
    mean_block = lax.dot_general(rows, piece_plain, contract, preferred_element_type=jnp.float32)
    delta_block = lax.dot_general(
        signed, piece_signed, contract, preferred_element_type=jnp.float32
    )
    grad_mean_acc = mean_block
    grad_delta_acc = delta_block
    result = (grad_rows, grad_signed, grad_mean_acc, grad_delta_acc)
    grad_rows, grad_signed, grad_mean_acc, grad_delta_acc = result
    slot_grad = (grad_rows + input_cols * grad_signed).astype(jnp.bfloat16)
    back = lax.all_to_all(
        slot_grad.reshape(width_local, experts, capacity),
        "expert",
        split_axis=1,
        concat_axis=1,
        tiled=True,
    )
    back = back.reshape(width_local, slots)
    grad_tokens = jnp.sum(jnp.take(back, slot_of, axis=1).astype(jnp.float32), axis=2).T.astype(
        jnp.bfloat16
    )
    grad_mean = grad_mean_acc.astype(jnp.bfloat16)[None]
    grad_rho = (grad_delta_acc * noise_float * jax.nn.sigmoid(rho_float)).astype(jnp.bfloat16)[None]
    return (hidden_out, grad_tokens, grad_mean, grad_rho)


def solution(mesh):
    in_specs = (
        P("expert", "dp"),
        P("expert", "dp"),
        P("expert", None),
        P("expert", None),
        P("expert", None),
        P("expert", "dp"),
        P("expert", "dp", None),
        P("expert", "dp", None),
        P("expert", "dp", None),
    )
    out_specs = (
        P("expert", "dp"),
        P("expert", "dp"),
        P("expert", "dp", None),
        P("expert", "dp", None),
    )
    return jax.shard_map(
        on_device, mesh=mesh, in_specs=in_specs, out_specs=out_specs, check_vma=False
    )
```

profile of v0, /device:TPU:1, one launch (start us, length us, event | category | flops | bytes accessed | tf_op | source)
XLA Modules:
  0.0 302.4 jit_solution(3396427842309068464)
XLA Ops:
  14.1 9.0 %all-to-all-start.1 = ((s32[8,1,440]{2,1,0:T(1,128)}), s32[8,1,440]{2,1,0:T(1,128)S(1)}, u32[]{:S(2)}, u32[]{:S(2)}) async-start(s32[8,1,440]{2,1,0:T(1,128)} %reshape.194), calls=%async_computation.1 | async-start | bytes 32768 | tf_op jit(solution)/shard_map/all_to_all | solution.py:75
  23.1 1.9 gather_fusion
  25.9 3.8 %all-to-all-done.1 = s32[8,1,440]{2,1,0:T(1,128)S(1)} async-done(((s32[8,1,440]{2,1,0:T(1,128)}), s32[8,1,440]{2,1,0:T(1,128)S(1)}, u32[]{:S(2)}, u32[]{:S(2)}) %all-to-all-start.1) | async-done | bytes 14112 | tf_op jit(solution)/shard_map/all_to_all | solution.py:75
  29.7 3.4 %all-to-all-start = ((bf16[8,40,128]{2,1,0:T(8,128)(2,1)}), bf16[8,40,128]{2,1,0:T(8,128)(2,1)S(1)}, u32[]{:S(2)}, u32[]{:S(2)}) async-start(bf16[8,40,128]{2,1,0:T(8,128)(2,1)} %select_multiply_fusion), calls=%async_computation | async-start | bytes 163840 | tf_op jit(solution)/shard_map/all_to_all | solution.py:74
  35.0 5.4 %all-to-all-done = bf16[8,40,128]{2,1,0:T(8,128)(2,1)S(1)} async-done(((bf16[8,40,128]{2,1,0:T(8,128)(2,1)}), bf16[8,40,128]{2,1,0:T(8,128)(2,1)S(1)}, u32[]{:S(2)}, u32[]{:S(2)}) %all-to-all-start) | async-done | bytes 81952 | tf_op jit(solution)/shard_map/all_to_all | solution.py:74
  40.4 1.3 convolution_bitcast_fusion
  42.4 2.9 fusion.28
  45.4 6.9 %pad_maximum_fusion = f32[7168,640]{0,1:T(8,128)} fusion(f32[7168,320]{0,1:T(8,128)S(1)} %fusion.28, f32[7168,320]{0,1:T(8,128)S(1)} %convolution_bitcast_fusion), kind=kLoop, calls=%fused_computation.5 | loop fusion | flops 4587520 | bytes 36700160 | tf_op jit(solution)/shard_map/concatenate | solution.py:94
  52.2 19.3 %copy.122 = f32[7168,640]{1,0:T(8,128)} copy(f32[7168,640]{0,1:T(8,128)} %pad_maximum_fusion) | data formatting | bytes 36700160
  72.4 2.0 gather_fusion.3
  75.5 3.4 %all-to-all-start.3 = ((bf16[224,8,40]{0,2,1:T(8,128)(2,1)}), bf16[224,8,40]{0,2,1:T(8,128)(2,1)S(1)}, u32[]{:S(2)}, u32[]{:S(2)}) async-start(bf16[224,8,40]{0,2,1:T(8,128)(2,1)} %multiply_convert_fusion.2), calls=%async_computation.3 | async-start | bytes 327680 | tf_op jit(solution)/shard_map/all_to_all | solution.py:112
  79.0 8.1 %all-to-all-done.3 = bf16[224,8,40]{0,2,1:T(8,128)(2,1)S(1)} async-done(((bf16[224,8,40]{0,2,1:T(8,128)(2,1)}), bf16[224,8,40]{0,2,1:T(8,128)(2,1)S(1)}, u32[]{:S(2)}, u32[]{:S(2)}) %all-to-all-start.3) | async-done | bytes 143392 | tf_op jit(solution)/shard_map/all_to_all | solution.py:112
  87.4 109.6 %reduce-scatter.4.cloned.1.call-done = f32[224,640]{1,0:T(8,128)} async-done(((f32[7168,640]{1,0:T(8,128)}), f32[224,640]{1,0:T(8,128)}) %reduce-scatter.4.cloned.1.call-update) | async-done | bytes 573456 | tf_op jit(solution)/shard_map/reduce_scatter | solution.py:93
  197.0 1.4 fusion.62
  199.3 1.3 multiply_convert_fusion.1
  201.4 6.7 %all-to-all-start.2 = ((bf16[224,8,40]{0,2,1:T(8,128)(2,1)}), bf16[224,8,40]{0,2,1:T(8,128)(2,1)S(1)}, u32[]{:S(2)}, u32[]{:S(2)}) async-start(bf16[224,8,40]{0,2,1:T(8,128)(2,1)} %bitcast.11), calls=%async_computation.2 | async-start | bytes 327680 | tf_op jit(solution)/shard_map/all_to_all | solution.py:100
  208.8 7.7 %all-to-all-done.2 = bf16[224,8,40]{0,2,1:T(8,128)(2,1)S(1)} async-done(((bf16[224,8,40]{0,2,1:T(8,128)(2,1)}), bf16[224,8,40]{0,2,1:T(8,128)(2,1)S(1)}, u32[]{:S(2)}, u32[]{:S(2)}) %all-to-all-start.2) | async-done | bytes 143392 | tf_op jit(solution)/shard_map/all_to_all | solution.py:100
  217.8 1.3 multiply_reduce_fusion
  219.8 41.2 %all-gather.2.cloned.1.call-done = bf16[7168,640]{1,0:T(8,128)(2,1)} async-done(((bf16[224,640]{1,0:T(8,128)(2,1)}), bf16[7168,640]{1,0:T(8,128)(2,1)}) %all-gather.2.cloned.1.call-update) | async-done | bytes 9175056 | tf_op jit(solution)/shard_map/all_gather | solution.py:13
  261.0 4.3 %fusion.34 = f32[128,320]{0,1:T(8,128)S(1)} fusion(bf16[1,128,7168]{2,1,0:T(8,128)(2,1)S(1)} %copy-done, bf16[7168,640]{1,0:T(8,128)(2,1)} %all-gather.2.cloned.1.call-done), kind=kOutput, calls=%fused_computation.48 | convolution fusion | flops 587202560 | bytes 7503872 | tf_op jit(solution)/shard_map/dot_general | solution.py:122
  265.4 7.8 %fusion.49 = bf16[128,320]{0,1:T(8,128)(2,1)} fusion(f32[128,320]{0,1:T(8,128)S(1)} %fusion.34, bf16[7168,640]{1,0:T(8,128)(2,1)} %all-gather.2.cloned.1.call-done, bf16[1,128,7168]{2,1,0:T(8,128)(2,1)S(1)} %copy-done.2, bf16[1,128,7168]{2,1,0:T(8,128)(2,1)S(1)} %copy-done.4, s32[128,320]{0,1:T(8,128)S(1)} %copy.119, s32[128]{0:T(128)S(1)} %shift_right_arithmetic.74), kind=kOutput, calls=%fused_computation.51 | convolution fusion | flops 596705280 | bytes 9585152 | tf_op jit(solution)/shard_map/dot_general | solution.py:123
  273.2 6.7 %all-to-all-start.4 = ((bf16[128,8,40]{0,2,1:T(8,128)(2,1)}), bf16[128,8,40]{0,2,1:T(8,128)(2,1)S(1)}, u32[]{:S(2)}, u32[]{:S(2)}) async-start(bf16[128,8,40]{0,2,1:T(8,128)(2,1)} %bitcast.22), calls=%async_computation.4 | async-start | bytes 163840 | tf_op jit(solution)/shard_map/all_to_all | solution.py:133
  280.0 8.2 %fusion.3 = bf16[1,128,7168]{2,1,0:T(8,128)(2,1)} fusion(bf16[7168,640]{1,0:T(8,128)(2,1)} %all-gather.2.cloned.1.call-done, bf16[1,128,7168]{2,1,0:T(8,128)(2,1)} %param.17, bf16[1,128,7168]{2,1,0:T(8,128)(2,1)} %param.16, bf16[320,128]{1,0:T(8,128)(2,1)S(1)} %bitcast.140, s32[320,128]{1,0:T(8,128)S(1)} %copy.120, s32[128]{0:T(128)S(1)} %shift_right_arithmetic.74), kind=kOutput, calls=%fused_computation.14 | convolution fusion | flops 594952192 | bytes 11256320 | tf_op jit(solution)/shard_map/dot_general | solution.py:125
  288.2 5.7 %fusion.2 = bf16[1,128,7168]{2,1,0:T(8,128)(2,1)} fusion(bf16[320,128]{1,0:T(8,128)(2,1)S(1)} %bitcast.141, bf16[7168,640]{1,0:T(8,128)(2,1)} %all-gather.2.cloned.1.call-done), kind=kOutput, calls=%fused_computation.13 | convolution fusion | flops 588120064 | bytes 7421952 | tf_op jit(solution)/shard_map/dot_general | solution.py:124
  (83 shorter events, 18.7 us)
Async XLA Ops:
  7.2 33.2 %copy-start = (bf16[1,128,7168]{2,1,0:T(8,128)(2,1)S(1)}, bf16[1,128,7168]{2,1,0:T(8,128)(2,1)}, u32[]{:S(2)}) copy-start(bf16[1,128,7168]{2,1,0:T(8,128)(2,1)} %param.15) | copy-start | bytes 5505028
  14.1 15.6 %all-to-all-start.1 = ((s32[8,1,440]{2,1,0:T(1,128)}), s32[8,1,440]{2,1,0:T(1,128)S(1)}, u32[]{:S(2)}, u32[]{:S(2)}) async-start(s32[8,1,440]{2,1,0:T(1,128)} %reshape.194), calls=%async_computation.1 | async-start | bytes 32768 | tf_op jit(solution)/shard_map/all_to_all | solution.py:75
  29.7 10.7 %all-to-all-start = ((bf16[8,40,128]{2,1,0:T(8,128)(2,1)}), bf16[8,40,128]{2,1,0:T(8,128)(2,1)S(1)}, u32[]{:S(2)}, u32[]{:S(2)}) async-start(bf16[8,40,128]{2,1,0:T(8,128)(2,1)} %select_multiply_fusion), calls=%async_computation | async-start | bytes 163840 | tf_op jit(solution)/shard_map/all_to_all | solution.py:74
  33.1 163.9 %reduce-scatter.4.cloned.1.call-start = ((), (), s32[]{:S(2)}) async-start(), calls=%async_computation.7 | async-start | bytes 18923520 | tf_op jit(solution)/shard_map/reduce_scatter | solution.py:93
  40.4 1.5 copy-start.1
  40.4 2.1 copy-start.3
  71.5 0.8 copy-start.5
  71.5 3.0 copy-start.6
  75.5 11.7 %all-to-all-start.3 = ((bf16[224,8,40]{0,2,1:T(8,128)(2,1)}), bf16[224,8,40]{0,2,1:T(8,128)(2,1)S(1)}, u32[]{:S(2)}, u32[]{:S(2)}) async-start(bf16[224,8,40]{0,2,1:T(8,128)(2,1)} %multiply_convert_fusion.2), calls=%async_computation.3 | async-start | bytes 327680 | tf_op jit(solution)/shard_map/all_to_all | solution.py:112
  78.9 182.1 %all-gather.2.cloned.1.call-start = ((), (), s32[]{:S(2)}) async-start(), calls=%async_computation.6 | async-start | bytes 9461760 | tf_op jit(solution)/shard_map/all_gather | solution.py:13
  201.4 15.1 %all-to-all-start.2 = ((bf16[224,8,40]{0,2,1:T(8,128)(2,1)}), bf16[224,8,40]{0,2,1:T(8,128)(2,1)S(1)}, u32[]{:S(2)}, u32[]{:S(2)}) async-start(bf16[224,8,40]{0,2,1:T(8,128)(2,1)} %bitcast.11), calls=%async_computation.2 | async-start | bytes 327680 | tf_op jit(solution)/shard_map/all_to_all | solution.py:100
  261.0 4.3 %copy-start.2 = (bf16[1,128,7168]{2,1,0:T(8,128)(2,1)S(1)}, bf16[1,128,7168]{2,1,0:T(8,128)(2,1)}, u32[]{:S(2)}) copy-start(bf16[1,128,7168]{2,1,0:T(8,128)(2,1)} %param.17) | copy-start | bytes 5505028
  261.0 4.4 %copy-start.4 = (bf16[1,128,7168]{2,1,0:T(8,128)(2,1)S(1)}, bf16[1,128,7168]{2,1,0:T(8,128)(2,1)}, u32[]{:S(2)}) copy-start(bf16[1,128,7168]{2,1,0:T(8,128)(2,1)} %param.16) | copy-start | bytes 5505028
  273.2 20.6 %all-to-all-start.4 = ((bf16[128,8,40]{0,2,1:T(8,128)(2,1)}), bf16[128,8,40]{0,2,1:T(8,128)(2,1)S(1)}, u32[]{:S(2)}, u32[]{:S(2)}) async-start(bf16[128,8,40]{0,2,1:T(8,128)(2,1)} %bitcast.22), calls=%async_computation.4 | async-start | bytes 163840 | tf_op jit(solution)/shard_map/all_to_all | solution.py:133
Sparse Core Ops, SparseCore 0:
  71.6 125.2 reduce-scatter.3
  200.1 60.8 all-gather.1
where the time goes:
time: 304 us; the launch traced here: 302 us
  waiting for transfers between devices  176 us (58%)
  local copies, waits for them, and re-layouts  35.1 us (12%)
  matrix products  30.3 us (10%)
  starting transfers between devices  29.3 us (10%)
  other arithmetic  17.5 us (6%)
  between operations  14.4 us (5%)
    reduce_scatter x1, waiting for transfers between devices, on_device(): lax.psum_scatter(jnp.concatenate([mean_part, pert_part], axis=1), 'dp', s...  110 us
    all_gather x1, waiting for transfers between devices, in_one_piece(): lax.all_gather(both, axis, axis=dim, tiled=True)  41.2 us
    unnamed x21, local copies, waits for them, and re-layouts  23.4 us
    all_to_all x1, starting transfers between devices, on_device(): lax.all_to_all(send_words, 'expert', split_axis=0, concat_axis=0, tiled=T...  9 us
    dot_general x1, matrix products, on_device(): lax.dot_general(signed, piece_signed, contract, preferred_element_type=jn...  8.23 us
    all_to_all x1, waiting for transfers between devices, on_device(): lax.all_to_all(upstream, 'expert', split_axis=1, concat_axis=1, tiled=True)  8.14 us
    dot_general x1, matrix products, on_device(): jnp.dot(delta_cols, piece_signed, preferred_element_type=jnp.float32)  7.84 us
    all_to_all x1, waiting for transfers between devices, on_device(): lax.all_to_all(hidden_slots.reshape(hidden_local, experts, capacity), 'ex...  7.72 us
  transfers between devices with their start and end apart: 7, of which 6 were waited for; matrix products, arithmetic and copies ran while one was open for 9% of the time, Pallas kernels for 0%

commit v1 on v0

v1 whole, which is shorter than its diff:
```python
import jax
import jax.numpy as jnp
from jax import lax
from jax.sharding import PartitionSpec as P

F32 = jnp.float32
BF16 = jnp.bfloat16
NT = (((1,), (1,)), ((), ()))
TN = (((0,), (0,)), ((), ()))


def dot(a, b, dims=(((1,), (0,)), ((), ()))):
    return lax.dot_general(a, b, dims, preferred_element_type=F32)


def unpack_rows(words):
    shifts = jnp.arange(32, dtype=jnp.int32)
    bits = jnp.bitwise_and(jnp.right_shift(words[..., None], shifts), 1)
    return (1 - 2 * bits).astype(F32).reshape(words.shape[:-1] + (words.shape[-1] * 32,))


def bytes_of(words):
    parts = [jnp.bitwise_and(jnp.right_shift(words, 8 * j), 255) for j in range(4)]
    return jnp.concatenate(parts, axis=1).astype(F32).astype(BF16)


def words_of(parts):
    n = parts.shape[1] // 4
    out = parts[:, :n].astype(jnp.int32)
    for j in range(1, 4):
        out = out | (parts[:, j * n:(j + 1) * n].astype(jnp.int32) << (8 * j))
    return out


def on_device(tokens, in_signs, out_signs, expert_ids, route_weight, cotangent,
              mean_weight, rho_weight, noise_weight):
    experts = lax.axis_size("expert")
    token_count, width = tokens.shape
    topk = expert_ids.shape[1]
    capacity = 5 * token_count * topk // (4 * experts)
    slots = experts * capacity
    hidden_local = cotangent.shape[1]
    in_words = in_signs.shape[1]

    flat_ids = expert_ids.reshape(-1)
    pairs = token_count * topk
    onehot = (flat_ids[:, None] == jnp.arange(experts, dtype=jnp.int32)).astype(BF16)
    lower = (jnp.arange(pairs)[:, None] > jnp.arange(pairs)[None, :]).astype(BF16)
    before = dot(lower, onehot)
    ranks = jnp.sum(before * onehot.astype(F32), axis=1).astype(jnp.int32)
    slot_of = (flat_ids * capacity + ranks).reshape(token_count, topk)
    slot_ids = jnp.arange(slots, dtype=jnp.int32)
    picks = [slot_of[:, k][:, None] == slot_ids[None, :] for k in range(topk)]
    pick = [p.astype(BF16) for p in picks]
    gather = sum(pick[1:], pick[0])
    slot_weight = sum(
        jnp.sum(jnp.where(p, route_weight[:, k][:, None], 0.0), axis=0)
        for k, p in enumerate(picks)
    )

    words = jnp.concatenate([in_signs, out_signs], axis=1)
    send_rows = dot(gather, tokens, TN).astype(BF16)
    send_cot = dot(gather, cotangent, TN) * slot_weight[:, None]
    send_words = words_of(dot(gather, bytes_of(words), TN))
    send = jnp.concatenate([send_rows, send_cot.astype(BF16)], axis=1)
    recv = lax.all_to_all(send.reshape(experts, capacity, -1), "expert", 0, 0, tiled=True)
    recv_words = lax.all_to_all(
        send_words.reshape(experts, capacity, -1), "expert", 0, 0, tiled=True)
    recv = recv.reshape(slots, -1)
    recv_words = recv_words.reshape(slots, -1)
    rows = recv[:, :width]
    upstream = recv[:, width:].T
    in_s = unpack_rows(recv_words[:, :in_words])
    signed = rows * in_s.astype(BF16)
    wt = recv_words[:, in_words:].T
    bit = (wt[:, None, :] >> jnp.arange(32, dtype=jnp.int32)[None, :, None]) & 1
    flip = bit.reshape(-1, slots)
    r_all = (1 - 2 * flip).astype(BF16)

    mean = mean_weight[0]
    rho = rho_weight[0].astype(F32)
    noise = noise_weight[0].astype(F32)
    delta = (jax.nn.softplus(rho) * noise).astype(BF16)
    part = dot(mean, rows, (((0,), (1,)), ((), ())))
    pert = dot(delta, signed, (((0,), (1,)), ((), ())))
    part = (part + pert * r_all.astype(F32)).astype(BF16)
    preact = lax.psum_scatter(part, "dp", scatter_dimension=0, tiled=True).astype(F32)
    gate = jax.nn.sigmoid(preact)
    hidden = (preact * gate).astype(BF16)
    slope = gate * (1.0 + preact * (1.0 - gate))
    dy_local = (upstream.astype(F32) * slope).astype(BF16)
    hid = lax.all_to_all(hidden.T.reshape(experts, capacity, -1), "expert", 0, 0, tiled=True)
    hid = hid.reshape(slots, -1)
    hidden_out = sum(
        dot(pick[k], hid) * route_weight[:, k][:, None] for k in range(topk)
    ).astype(BF16)

    dy = lax.all_gather(dy_local, "dp", axis=0, tiled=True)
    dyr = dy * r_all
    back = dot(mean, dy) + in_s.T * dot(delta, dyr)
    back = back.T.astype(BF16)
    ret = lax.all_to_all(back.reshape(experts, capacity, -1), "expert", 0, 0, tiled=True)
    grad_tokens = dot(gather, ret.reshape(slots, -1)).astype(BF16)
    grad_mean = dot(rows, dy, (((0,), (1,)), ((), ()))).astype(BF16)[None]
    gdelta = dot(signed, dyr, (((0,), (1,)), ((), ())))
    grad_rho = (gdelta * noise * jax.nn.sigmoid(rho)).astype(BF16)[None]
    return hidden_out, grad_tokens, grad_mean, grad_rho


def solution(mesh):
    row = P("expert", "dp")
    full = P("expert", None)
    weight = P("expert", "dp", None)
    return jax.shard_map(
        on_device, mesh=mesh,
        in_specs=(row, row, full, full, full, row, weight, weight, weight),
        out_specs=(row, row, weight, weight), check_vma=False)
```

time: 304 us -> 289 us (0.951)
  waiting for transfers between devices: 176 us -> 145 us
  blocking collectives: 0 us -> 14.9 us
  local copies, waits for them, and re-layouts: 35.1 us -> 49.7 us
  starting transfers between devices: 29.3 us -> 19.3 us
  other arithmetic: 17.5 us -> 9.89 us
  matrix products: 30.3 us -> 34.9 us
    reduce_scatter x1 -> x0, waiting for transfers between devices: 110 us -> none  [on_device(): lax.psum_scatter(jnp.concatenate([mean_part, pert_part], axis=1), 'dp', s...]
    unnamed x2 -> x3, waiting for transfers between devices: 0.03 us -> 91.1 us
    shift_right_arithmetic x4, local copies, waits for them, and re-layouts: 0.2 us -> 16.4 us  [on_device(): bit = wt[:, None, :] >> jnp.arange(32, dtype=jnp.int32)[None, :, None] & 1]
    all_to_all x0 -> x1, blocking collectives: none -> 14.9 us  [on_device(): lax.all_to_all(hidden.T.reshape(experts, capacity, -1), 'expert', 0, 0, t...]
    all_to_all x5 -> x3, starting transfers between devices: 29.2 us -> 19.2 us  [the longest x1 9.01 us: on_device(): lax.all_to_all(send.reshape(experts, capacity, -1), 'expert', 0, 0, tiled...]
    all_to_all x5 -> x3, waiting for transfers between devices: 25 us -> 15.2 us  [the longest x1 7.76 us: on_device(): lax.all_to_all(send.reshape(experts, capacity, -1), 'expert', 0, 0, tiled...]
    all_gather x0 -> x1, local copies, waits for them, and re-layouts: none -> 7.76 us  [on_device(): dy = lax.all_gather(dy_local, 'dp', axis=0, tiled=True)]
    concatenate x3 -> x1, other arithmetic: 8.38 us -> 0.73 us  [on_device(): send = jnp.concatenate([send_rows, send_cot.astype(BF16)], axis=1)]
  transfers between devices with their start and end apart: 7 -> 5, of which waited for: 6 -> 5; matrix products, arithmetic and copies ran while one was open for 9% -> 5% of each run, Pallas kernels for 0% -> 0%
where the time goes in v1:
time: 289 us; the launch traced here: 288 us
  waiting for transfers between devices  145 us (50%)
  local copies, waits for them, and re-layouts  49.7 us (17%)
  matrix products  34.9 us (12%)
  starting transfers between devices  19.3 us (7%)
  blocking collectives  14.9 us (5%)
  between operations  14.3 us (5%)
  other arithmetic  9.89 us (3%)
    unnamed x3, waiting for transfers between devices  91.1 us
    all_gather x1, waiting for transfers between devices, on_device(): dy = lax.all_gather(dy_local, 'dp', axis=0, tiled=True)  39 us
    dot_general x13, matrix products, dot(): return lax.dot_general(a, b, dims, preferred_element_type=F32)  34.9 us
    unnamed x24, local copies, waits for them, and re-layouts  24.1 us
    shift_right_arithmetic x4, local copies, waits for them, and re-layouts, on_device(): bit = wt[:, None, :] >> jnp.arange(32, dtype=jnp.int32)[None, :, None] & 1  16.4 us
    all_to_all x1, blocking collectives, on_device(): lax.all_to_all(hidden.T.reshape(experts, capacity, -1), 'expert', 0, 0, t...  14.9 us
    all_to_all x1, starting transfers between devices, on_device(): lax.all_to_all(send.reshape(experts, capacity, -1), 'expert', 0, 0, tiled...  9.01 us
    all_to_all x1, waiting for transfers between devices, on_device(): lax.all_to_all(send.reshape(experts, capacity, -1), 'expert', 0, 0, tiled...  7.76 us
  transfers between devices with their start and end apart: 5, of which 5 were waited for; matrix products, arithmetic and copies ran while one was open for 5% of the time, Pallas kernels for 0%

profile of v1, /device:TPU:1, one launch (start us, length us, event | category | flops | bytes accessed | tf_op | source)
XLA Modules:
  0.0 288.2 jit_solution(9468701827276511723)
XLA Ops:
  11.3 1.0 fusion.20
  13.0 9.0 %all-to-all-start = ((bf16[8,40,352]{2,1,0:T(8,128)(2,1)}), bf16[8,40,352]{2,1,0:T(8,128)(2,1)S(1)}, u32[]{:S(2)}, u32[]{:S(2)}) async-start(bf16[8,40,352]{2,1,0:T(8,128)(2,1)} %bitcast.4), calls=%async_computation | async-start | bytes 491520 | tf_op jit(solution)/shard_map/all_to_all | solution.py:66
  23.3 1.1 fusion.43
  24.4 7.8 %all-to-all-done = bf16[8,40,352]{2,1,0:T(8,128)(2,1)S(1)} async-done(((bf16[8,40,352]{2,1,0:T(8,128)(2,1)}), bf16[8,40,352]{2,1,0:T(8,128)(2,1)S(1)}, u32[]{:S(2)}, u32[]{:S(2)}) %all-to-all-start) | async-done | bytes 225312 | tf_op jit(solution)/shard_map/all_to_all | solution.py:66
  32.1 3.4 %all-to-all-start.1 = ((s32[8,40,228]{2,1,0:T(8,128)}), s32[8,40,228]{2,1,0:T(8,128)S(1)}, u32[]{:S(2)}, u32[]{:S(2)}) async-start(s32[8,40,228]{2,1,0:T(8,128)} %bitcast.11), calls=%async_computation.1 | async-start | bytes 655360 | tf_op jit(solution)/shard_map/all_to_all | solution.py:67
  35.8 4.8 %convolution_bitcast_fusion = f32[7168,320]{0,1:T(8,128)} fusion(bf16[1,128,7168]{2,1,0:T(8,128)(2,1)S(1)} %copy-done, bf16[320,352]{1,0:T(8,128)(2,1)S(1)} %bitcast.69), kind=kOutput, calls=%fused_computation.3 | convolution fusion | flops 587202560 | bytes 11091968 | tf_op jit(solution)/shard_map/dot_general | solution.py:13
  40.7 4.9 %all-to-all-done.1 = s32[8,40,228]{2,1,0:T(8,128)S(1)} async-done(((s32[8,40,228]{2,1,0:T(8,128)}), s32[8,40,228]{2,1,0:T(8,128)S(1)}, u32[]{:S(2)}, u32[]{:S(2)}) %all-to-all-start.1) | async-done | bytes 291872 | tf_op jit(solution)/shard_map/all_to_all | solution.py:67
  46.1 4.9 %shift_right_arithmetic.78 = s32[224,32,320]{2,1,0:T(8,128)} broadcast(s32[224,320]{1,0:T(8,128)S(1)} %bitcast.77), dimensions={0,2} | broadcast | bytes 9461760 | tf_op jit(solution)/shard_map/shift_right_arithmetic | solution.py:76
  51.0 11.4 %copy.50 = s32[7168,320]{0,1:T(8,128)} copy(s32[7168,320]{1,0:T(8,128)} %bitcast.66) | data formatting | bytes 18350080 | tf_op jit(solution)/shard_map/shift_right_arithmetic | solution.py:76
  62.5 5.4 %subtract_convert_fusion = bf16[7168,320]{0,1:T(8,128)(2,1)S(1)} fusion(s32[7168,320]{0,1:T(8,128)} %copy.50, s32[7168]{0:T(1024)S(1)} %shift_right_arithmetic.81), kind=kLoop, calls=%fused_computation.5 | loop fusion | flops 11468800 | bytes 13791232 | tf_op jit(solution)/shard_map/convert_element_type | solution.py:78
  67.9 2.1 copy-done.2
  69.9 7.7 %fusion.1 = bf16[7168,320]{0,1:T(8,128)(2,1)} fusion(f32[7168,320]{0,1:T(8,128)} %convolution_bitcast_fusion, bf16[320,128]{1,0:T(8,128)(2,1)S(1)} %fusion.58, bf16[7168,320]{0,1:T(8,128)(2,1)S(1)} %subtract_convert_fusion, bf16[1,128,7168]{2,1,0:T(8,128)(2,1)S(1)} %copy-done.3, bf16[1,128,7168]{2,1,0:T(8,128)(2,1)S(1)} %copy-done.5), kind=kOutput, calls=%fused_computation.4 | convolution fusion | flops 605552640 | bytes 22102016 | tf_op jit(solution)/shard_map/dot_general | solution.py:13
  77.6 7.5 %copy.52 = bf16[7168,320]{1,0:T(8,128)(2,1)} copy(bf16[7168,320]{0,1:T(8,128)(2,1)} %fusion.1) | data formatting | bytes 9175040
  85.2 91.1 %reduce-scatter.4.cloned.1.call-done = bf16[224,320]{1,0:T(8,128)(2,1)} async-done(((bf16[7168,320]{1,0:T(8,128)(2,1)}), bf16[224,320]{1,0:T(8,128)(2,1)}) %reduce-scatter.4.cloned.1.call-update) | async-done | bytes 143376
  178.2 14.9 %all_to_all.20 = bf16[8,40,224]{2,1,0:T(8,128)(2,1)S(1)} all-to-all(bf16[8,40,224]{2,1,0:T(8,128)(2,1)S(1)} %bitcast.79), channel_id=1, replica_groups=mesh['dp'=32,'expert'=8] {'expert'}, dimensions={0} | all-to-all | bytes 286720 | tf_op jit(solution)/shard_map/all_to_all | solution.py:92
  194.3 39.0 %all-gather.3.cloned.1.call-done = bf16[32,224,320]{1,2,0:T(8,128)(2,1)} async-done(((bf16[1,224,320]{1,2,0:T(8,128)(2,1)}), bf16[32,224,320]{1,2,0:T(8,128)(2,1)}) %all-gather.3.cloned.1.call-update) | async-done | bytes 4587536 | tf_op jit(solution)/shard_map/all_gather | solution.py:98
  233.3 7.8 %copy.51 = bf16[32,224,320]{1,0,2:T(8,128)(2,1)} copy(bf16[32,224,320]{1,2,0:T(8,128)(2,1)} %all-gather.3.cloned.1.call-done) | data formatting | bytes 9175040 | tf_op jit(solution)/shard_map/all_gather | solution.py:98
  241.0 11.5 %reshape.65 = bf16[7168,320]{0,1:T(8,128)(2,1)} reshape(bf16[32,224,320]{1,0,2:T(8,128)(2,1)} %copy.51) | data formatting | bytes 9175040
  252.5 8.2 %fusion.5 = bf16[1,128,7168]{2,1,0:T(8,128)(2,1)} fusion(bf16[320,128]{1,0:T(8,128)(2,1)S(1)} %fusion.58, bf16[1,128,7168]{2,1,0:T(8,128)(2,1)} %param.17, bf16[1,128,7168]{2,1,0:T(8,128)(2,1)} %param.16, bf16[7168,320]{0,1:T(8,128)(2,1)} %reshape.65, bf16[7168,320]{0,1:T(8,128)(2,1)} %copy-done.2), kind=kOutput, calls=%fused_computation.11 | convolution fusion | flops 596836352 | bytes 14761984 | tf_op jit(solution)/shard_map/dot_general | solution.py:13
  261.5 3.0 %fusion.24 = f32[320,128]{1,0:T(8,128)S(1)} fusion(bf16[7168,320]{0,1:T(8,128)(2,1)S(1)} %copy-done.1, bf16[7168,320]{0,1:T(8,128)(2,1)S(1)} %bitcast.68, s32[320,128]{1,0:T(8,128)S(1)} %copy.48, s32[128]{0:T(128)S(1)} %shift_right_arithmetic.75, bf16[1,128,7168]{2,1,0:T(8,128)(2,1)S(1)} %copy-done.4, bf16[1,128,7168]{2,1,0:T(8,128)(2,1)S(1)} %copy-done.6), kind=kOutput, calls=%fused_computation.33 | convolution fusion | flops 598917120 | bytes 13173248 | tf_op jit(solution)/shard_map/dot_general | solution.py:13
  264.5 2.0 fusion.27
  266.5 6.7 %all-to-all-start.3 = ((bf16[8,40,128]{2,1,0:T(8,128)(2,1)}), bf16[8,40,128]{2,1,0:T(8,128)(2,1)S(1)}, u32[]{:S(2)}, u32[]{:S(2)}) async-start(bf16[8,40,128]{2,1,0:T(8,128)(2,1)} %bitcast.21), calls=%async_computation.3 | async-start | bytes 163840 | tf_op jit(solution)/shard_map/all_to_all | solution.py:102
  273.2 4.7 %fusion.4 = bf16[1,128,7168]{2,1,0:T(8,128)(2,1)} fusion(bf16[7168,320]{0,1:T(8,128)(2,1)} %reshape.65, bf16[320,352]{1,0:T(8,128)(2,1)S(1)} %bitcast.72), kind=kOutput, calls=%fused_computation.10 | convolution fusion | flops 588120064 | bytes 6504448 | tf_op jit(solution)/shard_map/dot_general | solution.py:13
  277.9 2.6 all-to-all-done.3
  (53 shorter events, 11.7 us)
Async XLA Ops:
  7.2 28.7 %copy-start = (bf16[1,128,7168]{2,1,0:T(8,128)(2,1)S(1)}, bf16[1,128,7168]{2,1,0:T(8,128)(2,1)}, u32[]{:S(2)}) copy-start(bf16[1,128,7168]{2,1,0:T(8,128)(2,1)} %param.15) | copy-start | bytes 5505028
  13.0 19.1 %all-to-all-start = ((bf16[8,40,352]{2,1,0:T(8,128)(2,1)}), bf16[8,40,352]{2,1,0:T(8,128)(2,1)S(1)}, u32[]{:S(2)}, u32[]{:S(2)}) async-start(bf16[8,40,352]{2,1,0:T(8,128)(2,1)} %bitcast.4), calls=%async_computation | async-start | bytes 491520 | tf_op jit(solution)/shard_map/all_to_all | solution.py:66
  32.1 13.4 %all-to-all-start.1 = ((s32[8,40,228]{2,1,0:T(8,128)}), s32[8,40,228]{2,1,0:T(8,128)S(1)}, u32[]{:S(2)}, u32[]{:S(2)}) async-start(s32[8,40,228]{2,1,0:T(8,128)} %bitcast.11), calls=%async_computation.1 | async-start | bytes 655360 | tf_op jit(solution)/shard_map/all_to_all | solution.py:67
  35.6 140.7 %reduce-scatter.4.cloned.1.call-start = ((), (), s32[]{:S(2)}) async-start(), calls=%async_computation.6 | async-start | bytes 5677056
  62.4 7.5 %copy-start.3 = (bf16[1,128,7168]{2,1,0:T(8,128)(2,1)S(1)}, bf16[1,128,7168]{2,1,0:T(8,128)(2,1)}, u32[]{:S(2)}) copy-start(bf16[1,128,7168]{2,1,0:T(8,128)(2,1)} %param.17) | copy-start | bytes 5505028
  62.5 7.5 %copy-start.5 = (bf16[1,128,7168]{2,1,0:T(8,128)(2,1)S(1)}, bf16[1,128,7168]{2,1,0:T(8,128)(2,1)}, u32[]{:S(2)}) copy-start(bf16[1,128,7168]{2,1,0:T(8,128)(2,1)} %param.16) | copy-start | bytes 5505028
  67.9 2.1 copy-start.2
  85.2 148.1 %all-gather.3.cloned.1.call-start = ((), (), s32[]{:S(2)}) async-start(), calls=%async_computation.5 | async-start | bytes 5406720 | tf_op jit(solution)/shard_map/all_gather | solution.py:98
  241.0 19.6 %slice-start = ((s8[4587520]{0:T(1024)(128)(4,1)}), s8[393216]{0:T(1024)(128)(4,1)S(1)}, s32[]{:S(2)}) async-start(s8[4587520]{0:T(1024)(128)(4,1)} %bitcast.67), calls=%async_computation.7 | async-start | bytes 786432
  252.5 8.2 %copy-start.1 = (bf16[7168,320]{0,1:T(8,128)(2,1)S(1)}, bf16[7168,320]{0,1:T(8,128)(2,1)}, u32[]{:S(2)}) copy-start(bf16[7168,320]{0,1:T(8,128)(2,1)} %reshape.65) | copy-start | bytes 13762564
  252.5 8.2 %slice-start.1 = ((s8[4587520]{0:T(1024)(128)(4,1)}), s8[4194304]{0:T(1024)(128)(4,1)S(1)}, s32[]{:S(2)}) async-start(s8[4587520]{0:T(1024)(128)(4,1)} %bitcast.67), calls=%async_computation.8 | async-start | bytes 8388608
  252.5 8.2 %copy-start.4 = (bf16[1,128,7168]{2,1,0:T(8,128)(2,1)S(1)}, bf16[1,128,7168]{2,1,0:T(8,128)(2,1)}, u32[]{:S(2)}) copy-start(bf16[1,128,7168]{2,1,0:T(8,128)(2,1)} %param.17) | copy-start | bytes 5505028
  252.5 9.0 %copy-start.6 = (bf16[1,128,7168]{2,1,0:T(8,128)(2,1)S(1)}, bf16[1,128,7168]{2,1,0:T(8,128)(2,1)}, u32[]{:S(2)}) copy-start(bf16[1,128,7168]{2,1,0:T(8,128)(2,1)} %param.16) | copy-start | bytes 5505028
  266.5 14.0 %all-to-all-start.3 = ((bf16[8,40,128]{2,1,0:T(8,128)(2,1)}), bf16[8,40,128]{2,1,0:T(8,128)(2,1)S(1)}, u32[]{:S(2)}, u32[]{:S(2)}) async-start(bf16[8,40,128]{2,1,0:T(8,128)(2,1)} %bitcast.21), calls=%async_computation.3 | async-start | bytes 163840 | tf_op jit(solution)/shard_map/all_to_all | solution.py:102
Sparse Core Ops, SparseCore 0:
  85.3 90.9 reduce-scatter.3
  179.4 53.8 all-gather.2

commit v2 on v1

v2 whole, which is shorter than its diff:
```python
import functools

import jax
import jax.numpy as jnp
from jax import lax
from jax.experimental import pallas as pl
from jax.experimental.pallas import tpu as pltpu
from jax.sharding import PartitionSpec as P

F32 = jnp.float32
BF16 = jnp.bfloat16
I32 = jnp.int32
MESH = pl.DeviceIdType.MESH
NN = (((1,), (0,)), ((), ()))
TN = (((0,), (0,)), ((), ()))
VMEM = pl.BlockSpec(memory_space=pltpu.VMEM)

SIDE = 4
HALF = 112
OFFS = (2, 1, 3, 0)
CUT = ((0, 64), (64, 48))


def dot(a, b, dims=NN):
    return lax.dot_general(a, b, dims, preferred_element_type=F32)


def prep_kernel(mean_ref, rho_ref, noise_ref, wm_ref, wd_ref, vm_ref, vd_ref):
    delta = (jax.nn.softplus(rho_ref[...].astype(F32)) * noise_ref[...].astype(F32)).astype(BF16)
    for src, wt, w3 in ((mean_ref[...], wm_ref, vm_ref), (delta, wd_ref, vd_ref)):
        t = src.T
        for d in range(4):
            for h in range(2):
                at = (2 * d + h) * HALF
                wt[0, d * HALF:(d + 1) * HALF, h * 128:(h + 1) * 128] = t[at:at + HALF]
        w3[0] = wt[0].T


def prep(mean, rho, noise):
    blk = pl.BlockSpec((128, 896), lambda i: (0, i))
    tall = pl.BlockSpec((1, 448, 256), lambda i: (i, 0, 0))
    wide = pl.BlockSpec((1, 256, 448), lambda i: (i, 0, 0))
    return pl.pallas_call(
        prep_kernel,
        grid=(8,),
        in_specs=[blk, blk, blk],
        out_specs=[tall, tall, wide, wide],
        out_shape=[jax.ShapeDtypeStruct((8, 448, 256), BF16)] * 2
        + [jax.ShapeDtypeStruct((8, 256, 448), BF16)] * 2,
        cost_estimate=pl.CostEstimate(flops=40_000_000, bytes_accessed=13_000_000, transcendentals=2_000_000),
        name="weights",
    )(mean, rho, noise)


def swap_kernel(n, *refs):
    ins, outs, (send, recv) = refs[:n], refs[n:2 * n], refs[2 * n:]
    me = lax.axis_index("expert")
    barrier = pltpu.get_barrier_semaphore()
    for o in range(1, 8):
        pl.semaphore_signal(barrier, inc=1, device_id={"expert": lax.rem(me + o, 8)}, device_id_type=MESH)
    pl.semaphore_wait(barrier, 7)
    copies = []
    for i in range(n):
        for o in (4, 3, 5, 2, 6, 1, 7):
            to = lax.rem(me + o, 8)
            c = pltpu.make_async_remote_copy(
                ins[i].at[to], outs[i].at[me], send.at[i * 7 + o - 1], recv.at[i * 7 + o - 1],
                device_id={"expert": to}, device_id_type=MESH)
            c.start()
            copies.append(c)
    for i in range(n):
        outs[i][me] = ins[i][me]
    for c in copies:
        c.wait_recv()
    for c in copies:
        c.wait_send()


def swap(arrays, cid):
    n = len(arrays)
    return pl.pallas_call(
        functools.partial(swap_kernel, n),
        in_specs=[VMEM] * n,
        out_specs=[VMEM] * n,
        out_shape=[jax.ShapeDtypeStruct(a.shape, a.dtype) for a in arrays],
        scratch_shapes=[pltpu.SemaphoreType.DMA((7 * n,)), pltpu.SemaphoreType.DMA((7 * n,))],
        compiler_params=pltpu.CompilerParams(collective_id=cid, has_side_effects=True),
        name=f"swap{cid}",
    )(*arrays)


def sign_rows(l_ref, d, j):
    i = j // 2
    lane = lax.broadcasted_iota(I32, (1, 640), 1)
    if j % 2 == 0:
        row = jnp.where(lane < 320, l_ref[d, i:i + 1], l_ref[d, i:i + 1] >> 16)
    else:
        row = jnp.where(lane < 320, l_ref[d, i:i + 1] >> 16, l_ref[d, i + 1:i + 2])
    return (jnp.broadcast_to(row, (16, 640)) >> lax.broadcasted_iota(I32, (16, 640), 0)) & 1


def forward_kernel(wm_ref, wd_ref, l_ref, a_ref, b_ref, p_ref, m_ref, d_ref):
    m_ref[...] = dot(wm_ref[0], a_ref[...])
    d_ref[...] = dot(wd_ref[0], b_ref[...])
    for d in range(4):
        for j in range(7):
            at = d * HALF + 16 * j
            pert = d_ref[at:at + 16]
            pert = jnp.where(sign_rows(l_ref, d, j) != 0, -pert, pert)
            p_ref[d, 16 * j:16 * j + 16] = (m_ref[at:at + 16] + pert).astype(BF16)


def forward(wm, wd, lanes, a2, b2):
    tall = pl.BlockSpec((1, 448, 256), lambda i: (i, 0, 0))
    fixed = pl.BlockSpec((256, 640), lambda i: (0, 0))
    return pl.pallas_call(
        forward_kernel,
        grid=(8,),
        in_specs=[tall, tall, pl.BlockSpec((4, 4, 640), lambda i: (i, 0, 0)), fixed, fixed],
        out_specs=pl.BlockSpec((4, HALF, 640), lambda i: (i, 0, 0)),
        out_shape=jax.ShapeDtypeStruct((32, HALF, 640), BF16),
        scratch_shapes=[pltpu.VMEM((448, 640), F32), pltpu.VMEM((448, 640), F32)],
        name="products",
    )(wm, wd, lanes, a2, b2)


def ring_kernel(p_ref, up_ref, d_ref, h_ref, r0, q, t1, rp, rm, s, t2, rp2, rm2, send, recv):
    me = lax.axis_index("dp")
    k = lax.rem(me, 2)
    x, y = me // 8, lax.rem(me // 2, SIDE)
    a, b = x * (1 - k) + y * k, y * (1 - k) + x * k
    sa, sb = 8 - 6 * k, 2 + 6 * k
    partner = me + 1 - 2 * k

    def at(da, db):
        return lax.rem(a + da, SIDE) * sa + lax.rem(b + db, SIDE) * sb + k

    up_a, down_a, up_b, down_b = at(1, 0), at(3, 0), at(0, 1), at(0, 3)
    barrier = pltpu.get_barrier_semaphore()
    for peer in (partner, up_a, down_a, up_b, down_b):
        pl.semaphore_signal(barrier, inc=1, device_id={"dp": peer}, device_id_type=MESH)
    pl.semaphore_wait(barrier, 5)

    copies = []

    def put(src, dst, to):
        i = len(copies)
        c = pltpu.make_async_remote_copy(
            src, dst, send.at[i], recv.at[i], device_id={"dp": to}, device_id_type=MESH)
        c.start()
        copies.append(c)
        return c

    pair = {}
    for g in range(4):
        for r in range(4):
            theirs = (lax.rem(b + OFFS[g], SIDE) * sb + lax.rem(a + OFFS[r], SIDE) * sa + (1 - k))
            pair[g, r] = put(p_ref.at[theirs], r0.at[4 * g + r], partner)

    def merge(g, r):
        pair[g, r].wait_recv()
        q[4 * g + r] = p_ref[at(OFFS[g], OFFS[r])] + r0[4 * g + r]

    def qq(g, r):
        return q.at[4 * g + r]

    far, plus, minus = {}, {}, {}
    for r in (0, 1, 2, 3):
        merge(0, r)
        far[r] = put(qq(0, r), t1.at[r], up_a if r in (0, 3) else down_a)
    merge(2, 0)
    minus[0] = put(qq(2, 0), rm.at[0], down_a)
    merge(1, 0)
    merge(1, 1)
    merge(2, 1)

    def relay(r):
        far[r].wait_recv()
        g = 1 if r in (0, 3) else 2
        q[4 * g + r] = q[4 * g + r] + t1[r]
        if g == 1:
            plus[r] = put(qq(1, r), rp.at[r], up_a)
        else:
            minus[r] = put(qq(2, r), rm.at[r], down_a)

    relay(0)
    plus[1] = put(qq(1, 1), rp.at[1], up_a)
    relay(1)
    merge(1, 2)
    plus[2] = put(qq(1, 2), rp.at[2], up_a)
    merge(2, 2)
    relay(2)
    merge(2, 3)
    minus[3] = put(qq(2, 3), rm.at[3], down_a)
    merge(1, 3)
    relay(3)
    for r in range(4):
        merge(3, r)

    def total(r):
        plus[r].wait_recv()
        minus[r].wait_recv()
        return q[12 + r].astype(F32) + rp[r].astype(F32) + rm[r].astype(F32)

    (o0, n0), (o1, n1) = CUT
    c0, c1 = pl.ds(o0, n0), pl.ds(o1, n1)
    s[0] = total(0).astype(BF16)
    far_up = put(s.at[0, c0], t2.at[c0], up_b)
    far_dn = put(s.at[0, c1], t2.at[c1], down_b)
    s[1] = total(1).astype(BF16)
    p1 = put(s.at[1, c1], rp2.at[c1], up_b)
    s[2] = total(2).astype(BF16)
    m1 = put(s.at[2, c0], rm2.at[c0], down_b)
    far_up.wait_recv()
    s[1, c0] = s[1, c0] + t2[c0]
    p2 = put(s.at[1, c0], rp2.at[c0], up_b)
    far_dn.wait_recv()
    s[2, c1] = s[2, c1] + t2[c1]
    m2 = put(s.at[2, c1], rm2.at[c1], down_b)
    own = total(3)
    for c in (p1, m1, p2, m2):
        c.wait_recv()
    pre = own + rp2[...].astype(F32) + rm2[...].astype(F32)
    gate = jax.nn.sigmoid(pre)
    h_ref[...] = (pre * gate).astype(BF16)
    slope = gate * (1.0 + pre * (1.0 - gate))
    d_ref[me] = (up_ref[...].astype(F32) * slope).astype(BF16)

    def hand(da, db):
        i = at(da, db)
        return put(d_ref.at[i], d_ref.at[i], partner)

    def spread(db):
        i = at(0, db)
        up = put(d_ref.at[i], d_ref.at[i], up_a)
        dn = put(d_ref.at[i], d_ref.at[i], down_a)
        hand(0, db)
        return up, dn

    b_up = put(d_ref.at[me], d_ref.at[me], up_b)
    b_dn = put(d_ref.at[me], d_ref.at[me], down_b)
    sent = {0: spread(0)}
    b_up.wait_recv()
    i = at(0, 3)
    f_up = put(d_ref.at[i, c0], d_ref.at[i, c0], up_b)
    b_dn.wait_recv()
    i = at(0, 1)
    f_dn = put(d_ref.at[i, c1], d_ref.at[i, c1], down_b)
    sent[3] = spread(3)
    sent[1] = spread(1)

    fwd = {}

    def arrive(db):
        up, dn = sent[db]
        up.wait_recv()
        if db in (0, 2):
            i = at(3, db)
            fwd[db] = put(d_ref.at[i], d_ref.at[i], up_a)
        hand(3, db)
        dn.wait_recv()
        if db in (1, 3):
            i = at(1, db)
            fwd[db] = put(d_ref.at[i], d_ref.at[i], down_a)
        hand(1, db)

    arrive(0)
    f_up.wait_recv()
    f_dn.wait_recv()
    sent[2] = spread(2)
    arrive(3)
    arrive(1)
    arrive(2)
    for db in (0, 3, 1, 2):
        fwd[db].wait_recv()
        hand(2, db)
    waited = set(map(id, list(pair.values()) + list(far.values()) + list(plus.values()) + list(minus.values())
                     + [far_up, far_dn, p1, m1, p2, m2, b_up, b_dn, f_up, f_dn] + list(fwd.values())
                     + [c for two in sent.values() for c in two]))
    for c in copies:
        if id(c) not in waited:
            c.wait_recv()
    for c in copies:
        c.wait_send()


COPIES = 16 + 12 + 6 + 2 + 2 + 8 + 4 + 16


def ring(part, up):
    blk = lambda n: pltpu.VMEM((n, HALF, 640), BF16)
    one = pltpu.VMEM((HALF, 640), BF16)
    return pl.pallas_call(
        ring_kernel,
        in_specs=[VMEM, VMEM],
        out_specs=[VMEM, VMEM],
        out_shape=[jax.ShapeDtypeStruct((32, HALF, 640), BF16), jax.ShapeDtypeStruct((HALF, 640), BF16)],
        scratch_shapes=[blk(16), blk(16), blk(4), blk(4), blk(4), blk(3), one, one, one,
                        pltpu.SemaphoreType.DMA((COPIES,)), pltpu.SemaphoreType.DMA((COPIES,))],
        compiler_params=pltpu.CompilerParams(
            collective_id=1, has_side_effects=True, vmem_limit_bytes=56 * 1024 * 1024),
        name="ring",
    )(part, up)


def backward_kernel(dy_ref, l_ref, a_ref, b_ref, vm_ref, vd_ref, rho_ref, noise_ref, s_ref,
                    gm_ref, gr_ref, g_ref, dyr, accm, accd):
    step = pl.program_id(0)

    @pl.when(step == 0)
    def _():
        accm[...] = jnp.zeros_like(accm)
        accd[...] = jnp.zeros_like(accd)

    for d in range(4):
        for j in range(7):
            at = d * HALF + 16 * j
            v = dy_ref[d, 16 * j:16 * j + 16].astype(F32)
            dyr[at:at + 16] = jnp.where(sign_rows(l_ref, d, j) != 0, -v, v).astype(BF16)
    dy = dy_ref[...].reshape(448, 640)
    accm[...] += dot(vm_ref[0], dy)
    accd[...] += dot(vd_ref[0], dyr[...])

    def unfold(g):
        return jnp.concatenate(
            [g[d * HALF:(d + 1) * HALF, h * 128:(h + 1) * 128] for d in range(4) for h in range(2)], axis=0)

    gm_ref[...] = unfold(dot(dy, a_ref[...])).T.astype(BF16)
    gd = unfold(dot(dyr[...], b_ref[...])).T
    gr_ref[...] = (gd * noise_ref[...].astype(F32) * jax.nn.sigmoid(rho_ref[...].astype(F32))).astype(BF16)

    @pl.when(step == 7)
    def _():
        plain = accm[0:128, 0:320] + accm[128:256, 320:640]
        pert = accd[0:128, 0:320] + accd[128:256, 320:640]
        g = (plain + s_ref[...] * pert).T
        for e in range(8):
            g_ref[e] = g[40 * e:40 * e + 40].astype(BF16)


def backward(dy, lanes, a3, b3, vm, vd, rho, noise, s_cols):
    blk = pl.BlockSpec((128, 896), lambda i: (0, i))
    wide = pl.BlockSpec((1, 256, 448), lambda i: (i, 0, 0))
    fixed = pl.BlockSpec((640, 256), lambda i: (0, 0))
    return pl.pallas_call(
        backward_kernel,
        grid=(8,),
        in_specs=[pl.BlockSpec((4, HALF, 640), lambda i: (i, 0, 0)),
                  pl.BlockSpec((4, 4, 640), lambda i: (i, 0, 0)), fixed, fixed, wide, wide, blk, blk,
                  pl.BlockSpec((128, 320), lambda i: (0, 0))],
        out_specs=[blk, blk, pl.BlockSpec((8, 40, 128), lambda i: (0, 0, 0))],
        out_shape=[jax.ShapeDtypeStruct((128, 7168), BF16)] * 2 + [jax.ShapeDtypeStruct((8, 40, 128), BF16)],
        scratch_shapes=[pltpu.VMEM((448, 640), BF16), pltpu.VMEM((256, 640), F32), pltpu.VMEM((256, 640), F32)],
        name="gradients",
    )(dy, lanes, a3, b3, vm, vd, rho, noise, s_cols)


def unpack_rows(words):
    bits = (words[..., None] >> jnp.arange(32, dtype=I32)) & 1
    return (1 - 2 * bits).astype(F32).reshape(words.shape[:-1] + (words.shape[-1] * 32,))


def bytes_of(words):
    parts = [(words >> (8 * j)) & 255 for j in range(4)]
    return jnp.concatenate(parts, axis=1).astype(F32).astype(BF16)


def words_of(parts):
    n = parts.shape[1] // 4
    ints = parts.astype(I32)
    return ints[:, :n] | (ints[:, n:2 * n] << 8) | (ints[:, 2 * n:3 * n] << 16) | (ints[:, 3 * n:] << 24)


def doubled(m):
    zero = jnp.zeros_like(m)
    return jnp.concatenate(
        [jnp.concatenate([m, zero], axis=1), jnp.concatenate([zero, m], axis=1)], axis=0)


def on_device(tokens, in_signs, out_signs, expert_ids, route_weight, cotangent,
              mean_weight, rho_weight, noise_weight):
    experts, capacity, slots, topk = 8, 40, 320, 2
    token_count = tokens.shape[0]

    wm, wd, vm, vd = prep(mean_weight[0], rho_weight[0], noise_weight[0])

    flat_ids = expert_ids.reshape(-1)
    pairs = token_count * topk
    onehot = (flat_ids[:, None] == jnp.arange(experts, dtype=I32)).astype(BF16)
    lower = (jnp.arange(pairs)[:, None] > jnp.arange(pairs)[None, :]).astype(BF16)
    before = dot(lower, onehot)
    ranks = jnp.sum(before * onehot.astype(F32), axis=1).astype(I32)
    slot_of = (flat_ids * capacity + ranks).reshape(token_count, topk)
    slot_ids = jnp.arange(slots, dtype=I32)
    picks = [slot_of[:, k][:, None] == slot_ids[None, :] for k in range(topk)]
    pick = [p.astype(BF16) for p in picks]
    gather = pick[0] + pick[1]
    slot_weight = sum(
        jnp.sum(jnp.where(p, route_weight[:, k][:, None], 0.0), axis=0) for k, p in enumerate(picks))

    send_rows = dot(gather, tokens, TN).astype(BF16)
    send_cot = (dot(gather, cotangent, TN) * slot_weight[:, None]).astype(BF16)
    send_words = words_of(dot(gather, bytes_of(jnp.concatenate([out_signs, in_signs], axis=1)), TN))
    rows, words, up = swap(
        [v.reshape(experts, capacity, -1) for v in (send_rows, send_words, send_cot)], 2)
    rows, words, up = (v.reshape(slots, -1) for v in (rows, words, up))

    in_s = unpack_rows(words[:, 224:])
    signed = rows * in_s.astype(BF16)
    wt = words[:, :224].T.reshape(32, 7, slots)
    lanes = jnp.concatenate([wt[:, 0:4], wt[:, 3:7]], axis=2)
    up2 = up.T
    up2 = jnp.concatenate([up2[:HALF], up2[HALF:]], axis=1)

    part = forward(wm, wd, lanes, doubled(rows.T), doubled(signed.T))
    dy, hid = ring(part, up2)
    grad_mean, grad_rho, g = backward(
        dy, lanes, doubled(rows), doubled(signed), vm, vd, rho_weight[0], noise_weight[0], in_s.T)
    hid = jnp.concatenate([hid[:, :slots], hid[:, slots:]], axis=0).T
    hid, back = swap([hid.reshape(experts, capacity, -1), g], 3)
    hid = hid.reshape(slots, -1)
    hidden_out = (dot(pick[0], hid) * route_weight[:, 0:1]
                  + dot(pick[1], hid) * route_weight[:, 1:2]).astype(BF16)
    grad_tokens = dot(gather, back.reshape(slots, -1)).astype(BF16)
    return hidden_out, grad_tokens, grad_mean[None], grad_rho[None]


def solution(mesh):
    row = P("expert", "dp")
    full = P("expert", None)
    weight = P("expert", "dp", None)
    return jax.shard_map(
        on_device, mesh=mesh,
        in_specs=(row, row, full, full, full, row, weight, weight, weight),
        out_specs=(row, row, weight, weight), check_vma=False)
```

time: 289 us -> 140 us (0.48)
  waiting for transfers between devices: 145 us -> 0 us
  Pallas kernels: 0 us -> 116 us
  local copies, waits for them, and re-layouts: 49.7 us -> 8.96 us
  matrix products: 34.9 us -> 6.98 us
  starting transfers between devices: 19.3 us -> 0 us
  blocking collectives: 14.9 us -> 0 us
  between operations: 14.3 us -> 0.84 us
    pallas_call x0 -> x6, Pallas kernels: none -> 116 us  [the longest x1 47.9 us: ring(): pl.pallas_call(ring_kernel, in_specs=[VMEM, VMEM], out_specs=[VMEM, VMEM]...]
    unnamed x3 -> x0, waiting for transfers between devices: 91.1 us -> none
    all_gather x1 -> x0, waiting for transfers between devices: 39 us -> none  [on_device(): dy = lax.all_gather(dy_local, 'dp', axis=0, tiled=True)]
    dot_general x13 -> x7, matrix products: 34.9 us -> 6.98 us  [dot(): return lax.dot_general(a, b, dims, preferred_element_type=F32)]
    unnamed x24 -> x13, local copies, waits for them, and re-layouts: 24.1 us -> 2.86 us
    all_to_all x3 -> x0, starting transfers between devices: 19.2 us -> none  [the longest x1 9.01 us: on_device(): lax.all_to_all(send.reshape(experts, capacity, -1), 'expert', 0, 0, tiled...]
    shift_right_arithmetic x8 -> x2, local copies, waits for them, and re-layouts: 16.6 us -> 0.09 us  [unpack_rows(): bits = words[..., None] >> jnp.arange(32, dtype=I32) & 1]
    all_to_all x3 -> x0, waiting for transfers between devices: 15.2 us -> none  [the longest x1 7.76 us: on_device(): lax.all_to_all(send.reshape(experts, capacity, -1), 'expert', 0, 0, tiled...]
  transfers between devices with their start and end apart: 5 -> 0, of which waited for: 5 -> 0; matrix products, arithmetic and copies ran while one was open for 5% -> 0% of each run, Pallas kernels for 0% -> 0%
where the time goes in v2:
time: 140 us; the launch traced here: 139 us
  Pallas kernels  116 us (83%)
  local copies, waits for them, and re-layouts  8.96 us (6%)
  other arithmetic  7.05 us (5%)
  matrix products  6.98 us (5%)
    pallas_call x1, Pallas kernels, ring(): pl.pallas_call(ring_kernel, in_specs=[VMEM, VMEM], out_specs=[VMEM, VMEM]...  47.9 us
    pallas_call x2, Pallas kernels, swap(): pl.pallas_call(functools.partial(swap_kernel, n), in_specs=[VMEM] * n, ou...  34.9 us
    pallas_call x1, Pallas kernels, backward(): pl.pallas_call(backward_kernel, grid=(8,), in_specs=[pl.BlockSpec((4, HAL...  13.8 us
    pallas_call x1, Pallas kernels, prep(): pl.pallas_call(prep_kernel, grid=(8,), in_specs=[blk, blk, blk], out_spec...  9.88 us
    pallas_call x1, Pallas kernels, forward(): pl.pallas_call(forward_kernel, grid=(8,), in_specs=[tall, tall, pl.BlockS...  9.25 us
    dot_general x7, matrix products, dot(): return lax.dot_general(a, b, dims, preferred_element_type=F32)  6.98 us
    unnamed x13, local copies, waits for them, and re-layouts  2.86 us

profile of v2, /device:TPU:1, one launch (start us, length us, event | category | flops | bytes accessed | tf_op | source)
XLA Modules:
  0.0 139.5 jit_solution(14570301577522675773)
XLA Ops:
  0.6 0.8 copy.50
  2.7 0.8 slice_bitcast_fusion
  3.7 0.9 fusion
  4.6 0.9 constant_dynamic-update-slice_fusion.1
  6.6 1.0 fusion.17
  7.6 0.8 convolution_convert_fusion.1
  8.4 23.3 %swap2.1 = (bf16[8,40,128]{2,1,0:T(8,128)(2,1)}, s32[8,40,228]{2,1,0:T(8,128)}, bf16[8,40,224]{2,1,0:T(8,128)(2,1)}) custom-call(bf16[8,40,128]{2,1,0:T(8,128)(2,1)} %bitcast.67, s32[8,40,228]{2,1,0:T(8,128)} %bitcast.53, bf16[8,40,224]{2,1,0:T(8,128)(2,1)} %bitcast.66), custom_call_target="tpu_custom_call" | custom-call | tf_op jit(solution)/shard_map/swap2/pallas_call | solution.py:81
  31.7 1.0 slice.73
  32.8 1.0 copy.53
  34.1 0.8 fusion.16.b_ref
  34.9 1.1 copy.59
  36.2 0.9 pad_add_fusion.l_ref
  37.1 0.8 fusion.15.a_ref
  37.9 9.9 %weights.1 = (bf16[8,448,256]{2,1,0:T(8,128)(2,1)}, bf16[8,448,256]{2,1,0:T(8,128)(2,1)}, bf16[8,256,448]{2,1,0:T(8,128)(2,1)}, bf16[8,256,448]{2,1,0:T(8,128)(2,1)}) custom-call(bf16[128,7168]{1,0:T(8,128)(2,1)} %bitcast.51, bf16[128,7168]{1,0:T(8,128)(2,1)} %bitcast.47, bf16[128,7168]{1,0:T(8,128)(2,1)} %bitcast.49), custom_call_target="tpu_custom_call" | custom-call | flops 40000000 | bytes 13000000 | tf_op jit(solution)/shard_map/weights/pallas_call | solution.py:43
  47.8 9.3 %products.1.p_ref = bf16[32,112,640]{2,1,0:T(8,128)(2,1)} custom-call(bf16[8,448,256]{2,1,0:T(8,128)(2,1)} %get-tuple-element.18.wm_ref, bf16[8,448,256]{2,1,0:T(8,128)(2,1)} %get-tuple-element.19.wd_ref, s32[32,4,640]{2,1,0:T(4,128)} %pad_add_fusion.l_ref, bf16[256,640]{1,0:T(8,128)(2,1)} %fusion.15.a_ref, bf16[256,640]{1,0:T(8,128)(2,1)} %fusion.16.b_ref), custom_call_target="tpu_custom_call" | custom-call | tf_op jit(solution)/shard_map/products/pallas_call | solution.py:116
  58.0 47.9 %ring.1 = (bf16[32,112,640]{2,1,0:T(8,128)(2,1)}, bf16[112,640]{1,0:T(8,128)(2,1)}) custom-call(bf16[32,112,640]{2,1,0:T(8,128)(2,1)} %products.1.p_ref, bf16[112,640]{1,0:T(8,128)(2,1)} %pad_maximum_fusion.up_ref), custom_call_target="tpu_custom_call" | custom-call | tf_op jit(solution)/shard_map/ring/pallas_call | solution.py:293
  106.0 0.9 copy.58.b_ref
  106.9 0.8 fusion.24
  108.4 13.8 %gradients.1 = (bf16[128,7168]{1,0:T(8,128)(2,1)}, bf16[128,7168]{1,0:T(8,128)(2,1)}, bf16[8,40,128]{2,1,0:T(8,128)(2,1)}) custom-call(bf16[32,112,640]{2,1,0:T(8,128)(2,1)} %get-tuple-element.24.dy_ref, s32[32,4,640]{2,1,0:T(4,128)} %pad_add_fusion.l_ref, bf16[640,256]{1,0:T(8,128)(2,1)} %fusion.14.a_ref, bf16[640,256]{1,0:T(8,128)(2,1)} %copy.58.b_ref, ...), custom_call_target="tpu_custom_call" | custom-call | tf_op jit(solution)/shard_map/gradients/pallas_call | solution.py:345
  122.3 0.8 copy.57
  123.1 11.6 %swap3.1 = (bf16[8,40,224]{2,1,0:T(8,128)(2,1)}, bf16[8,40,128]{2,1,0:T(8,128)(2,1)}) custom-call(bf16[8,40,224]{2,1,0:T(8,128)(2,1)} %bitcast.62, bf16[8,40,128]{2,1,0:T(8,128)(2,1)} %get-tuple-element.27.refs_1_), custom_call_target="tpu_custom_call" | custom-call | tf_op jit(solution)/shard_map/swap3/pallas_call | solution.py:81
  134.7 1.7 %convolution_convert_fusion.2 = bf16[128,128]{1,0:T(8,128)(2,1)} fusion(bf16[320,128]{1,0:T(8,128)(2,1)} %bitcast.70, s32[128]{0:T(128)S(1)} %get-tuple-element.45, s32[128]{0:T(128)S(1)} %get-tuple-element.44), kind=kOutput, calls=%fused_computation.8 | convolution fusion | flops 10829824 | bytes 115712 | tf_op jit(solution)/shard_map/dot_general | solution.py:25
  136.5 1.2 convolution_multiply_fusion.1
  137.7 1.8 %fusion.2 = bf16[128,224]{0,1:T(8,128)(2,1)} fusion(f32[128,224]{0,1:T(8,128)S(1)} %convolution_multiply_fusion.1, bf16[320,224]{1,0:T(8,128)(2,1)} %bitcast.61, s32[128]{0:T(128)S(1)} %get-tuple-element.44, f32[128]{0:T(128)S(1)} %get-tuple-element.43), kind=kOutput, calls=%fused_computation.7 | convolution fusion | flops 18477056 | bytes 316416 | tf_op jit(solution)/shard_map/dot_general | solution.py:25
  (35 shorter events, 4.9 us)
Async XLA Ops:
  0.6 3.0 %copy-start = (bf16[128,224]{0,1:T(8,128)(2,1)S(1)}, bf16[128,224]{0,1:T(8,128)(2,1)}, u32[]{:S(2)}) copy-start(bf16[128,224]{0,1:T(8,128)(2,1)} %param.14) | copy-start | bytes 172036
  6.2 1.4 %copy-start.4 = (bf16[128,128]{1,0:T(8,128)(2,1)S(1)}, bf16[128,128]{1,0:T(8,128)(2,1)}, u32[]{:S(2)}) copy-start(bf16[128,128]{1,0:T(8,128)(2,1)} %param.9) | copy-start | bytes 98308
  47.8 9.3 %copy-start.3 = (bf16[8,40,224]{2,1,0:T(8,128)(2,1)S(1)}, bf16[8,40,224]{2,1,0:T(8,128)(2,1)}, u32[]{:S(2)}) copy-start(bf16[8,40,224]{2,1,0:T(8,128)(2,1)} %get-tuple-element.22) | copy-start | bytes 430084
  58.0 49.7 %copy-start.1 = (bf16[8,40,128]{2,1,0:T(8,128)(2,1)S(1)}, bf16[8,40,128]{2,1,0:T(8,128)(2,1)}, u32[]{:S(2)}) copy-start(bf16[8,40,128]{2,1,0:T(8,128)(2,1)} %get-tuple-element.21) | copy-start | bytes 245764
  108.4 13.8 %copy-start.2 = (bf16[112,640]{1,0:T(8,128)(2,1)S(1)}, bf16[112,640]{1,0:T(8,128)(2,1)}, u32[]{:S(2)}) copy-start(bf16[112,640]{1,0:T(8,128)(2,1)} %get-tuple-element.23) | copy-start | bytes 430084

commit v3 on v1

v3 whole, which is shorter than its diff:
```python
import jax
import jax.numpy as jnp
from jax import lax
from jax.experimental import pallas as pl
from jax.experimental.pallas import tpu as pltpu
from jax.sharding import PartitionSpec as P

F32 = jnp.float32
BF16 = jnp.bfloat16
I32 = jnp.int32
MESH = pl.DeviceIdType.MESH
NN = (((1,), (0,)), ((), ()))
TN = (((0,), (0,)), ((), ()))
VMEM = pl.BlockSpec(memory_space=pltpu.VMEM)

SIDE = 4
HALF = 112
OFFS = (2, 1, 3, 0)
CUT = ((0, 64), (64, 48))


def dot(a, b, dims=NN):
    return lax.dot_general(a, b, dims, preferred_element_type=F32)


ZORDER = (4, 3, 5, 2, 6, 1, 7)
UNITS = 7168
BLOCK = 896
COPIES = 35 + 1 + 16 + 12 + 6 + 2 + 2 + 8 + 4 + 16


def layer_kernel(rows_in, words_in, cot_in, mean_hbm, rho_hbm, noise_hbm,
                 hid_out, back_out, gm_hbm, gr_hbm,
                 mean, rho, noise, wm, wd, rows_r, words_r, words_p, cot_r, w2, bda, bdb, ba, bb, sgn_t,
                 up2, mx, dx, p, r0, q, t1, rp, rm, s, t2, rp2, rm2, dbuf, hs, dyr, accm, accd,
                 gt, gdt, gs, gm, gr, send, recv, local):
    me, z = lax.axis_index("dp"), lax.axis_index("expert")
    k = lax.rem(me, 2)
    x, y = me // 8, lax.rem(me // 2, SIDE)
    a, b = x * (1 - k) + y * k, y * (1 - k) + x * k
    sa, sb = 8 - 6 * k, 2 + 6 * k
    partner = me + 1 - 2 * k

    def at(da, db):
        return lax.rem(a + da, SIDE) * sa + lax.rem(b + db, SIDE) * sb + k

    def theirs(db, da):
        return lax.rem(b + db, SIDE) * sb + lax.rem(a + da, SIDE) * sa + (1 - k)

    up_a, down_a, up_b, down_b = at(1, 0), at(3, 0), at(0, 1), at(0, 3)

    loads = [pltpu.make_async_copy(src, dst, local.at[16 + i]) for i, (src, dst) in enumerate(
        ((rho_hbm, rho), (noise_hbm, noise), (mean_hbm, mean)))]
    for c in loads:
        c.start()
    barrier = pltpu.get_barrier_semaphore()
    for o in ZORDER:
        pl.semaphore_signal(barrier, inc=1, device_id={"expert": lax.rem(z + o, 8)}, device_id_type=MESH)
    for peer in (up_a, down_a, up_b, down_b, partner):
        pl.semaphore_signal(barrier, inc=1, device_id={"dp": peer}, device_id_type=MESH)
    pl.semaphore_wait(barrier, 12)

    copies, done = [], set()

    def put(src, dst, to, axis="dp"):
        i = len(copies)
        c = pltpu.make_async_remote_copy(
            src, dst, send.at[i], recv.at[i], device_id={axis: to}, device_id_type=MESH)
        c.start()
        copies.append(c)
        return c

    def arrived(c):
        done.add(id(c))
        c.wait_recv()

    def swap(src, dst):
        out = []
        for o in ZORDER:
            to = lax.rem(z + o, 8)
            out.append(put(src.at[to], dst.at[z], to, "expert"))
        return out

    z_words = swap(words_in, words_r)
    z_rows = swap(rows_in, rows_r)
    z_cot = swap(cot_in, cot_r)
    words_r[z] = words_in[z]
    rows_r[z] = rows_in[z]
    cot_r[z] = cot_in[z]

    for c in loads:
        c.wait()

    def fold(i, carry):
        cols = pl.ds(pl.multiple_of(i * BLOCK, 128), BLOCK)
        delta = (jax.nn.softplus(rho[:, cols].astype(F32)) * noise[:, cols].astype(F32)).astype(BF16)
        for v, wt in ((mean[:, cols], wm), (delta, wd)):
            t = v.T
            for d in range(4):
                for h in range(2):
                    o = (2 * d + h) * HALF
                    wt[4 * i + d, :, h * 128:(h + 1) * 128] = t[o:o + HALF]
        return carry

    lax.fori_loop(0, 8, fold, 0)

    def slots_of(ref):
        return jnp.concatenate([ref[e].astype(F32) for e in range(8)], axis=0)

    for c in z_words:
        arrived(c)
    pair_words = put(words_r, words_p, partner)
    words = jnp.concatenate([words_r[e] for e in range(8)], axis=0)
    wt = words.T
    w2[k] = jnp.concatenate([wt, wt], axis=1)
    lane = lax.broadcasted_iota(I32, (320, 128), 1)
    word = jnp.broadcast_to(words[:, 115:116], (320, 128))
    for w in range(3):
        word = jnp.where(lane // 32 == w, jnp.broadcast_to(words[:, 112 + w:113 + w], (320, 128)), word)
    sgn = (1 - 2 * ((word >> (lane & 31)) & 1)).astype(F32)
    for c in z_rows:
        arrived(c)
    plain = slots_of(rows_r)
    signed = plain * sgn
    sgn_t[...] = sgn.T
    none_w, none_t = jnp.zeros((128, 320), F32), jnp.zeros((320, 128), F32)
    for v, wide, tall in ((plain, bda, ba), (signed, bdb, bb)):
        t = v.T
        wide[0:128] = jnp.concatenate([t, none_w], axis=1).astype(BF16)
        wide[128:256] = jnp.concatenate([none_w, t], axis=1).astype(BF16)
        tall[0:320] = jnp.concatenate([v, none_t], axis=1).astype(BF16)
        tall[320:640] = jnp.concatenate([none_t, v], axis=1).astype(BF16)
    arrived(pair_words)
    wt = jnp.concatenate([words_p[e] for e in range(8)], axis=0).T
    w2[1 - k] = jnp.concatenate([wt, wt], axis=1)

    left = lax.broadcasted_iota(I32, (1, 640), 1) < 320
    down16 = lax.broadcasted_iota(I32, (16, 640), 0)

    def minus_at(dd, j):
        half, base = dd // 16, lax.rem(dd, 16) * 7
        one = w2[half, pl.ds(base + j // 2, 1), :] >> (16 * (j % 2))
        two = w2[half, pl.ds(base + 3 + (j + 1) // 2, 1), :] >> (16 * ((j + 1) % 2))
        return ((jnp.broadcast_to(jnp.where(left, one, two), (16, 640)) >> down16) & 1) != 0

    def products(dd_of):
        mx[...] = dot(jnp.concatenate([wm[dd_of(r)] for r in range(4)], axis=0), bda[...])
        dx[...] = dot(jnp.concatenate([wd[dd_of(r)] for r in range(4)], axis=0), bdb[...])

        def combine(r, carry):
            dd = dd_of(r)
            for j in range(7):
                rows = pl.ds(pl.multiple_of(r * HALF + 16 * j, 16), 16)
                pert = dx[rows]
                p[dd, 16 * j:16 * j + 16] = (
                    mx[rows] + jnp.where(minus_at(dd, j), -pert, pert)).astype(BF16)
            return carry

        lax.fori_loop(0, 4, combine, 0)

    pair = {}

    def products_pair(g):
        products(lambda r: theirs(OFFS[g], r))
        for r in range(4):
            pair[g, r] = put(p.at[theirs(OFFS[g], OFFS[r])], r0.at[4 * g + r], partner)

    def products_own(g):
        products(lambda r: at(OFFS[g], r))

    def merge(g, r):
        arrived(pair[g, r])
        q[4 * g + r] = p[at(OFFS[g], OFFS[r])] + r0[4 * g + r]

    def qq(g, r):
        return q.at[4 * g + r]

    far, plus, minus = {}, {}, {}
    products_pair(0)
    products_own(0)
    products_pair(1)
    for r in range(4):
        merge(0, r)
        far[r] = put(qq(0, r), t1.at[r], up_a if r in (0, 3) else down_a)
    products_pair(2)
    products_own(1)
    products_own(2)

    def relay(r):
        arrived(far[r])
        g = 1 if r in (0, 3) else 2
        q[4 * g + r] = q[4 * g + r] + t1[r]
        if g == 1:
            plus[r] = put(qq(1, r), rp.at[r], up_a)
        else:
            minus[r] = put(qq(2, r), rm.at[r], down_a)

    merge(2, 0)
    minus[0] = put(qq(2, 0), rm.at[0], down_a)
    merge(1, 0)
    relay(0)
    merge(1, 1)
    plus[1] = put(qq(1, 1), rp.at[1], up_a)
    merge(2, 1)
    relay(1)
    merge(1, 2)
    plus[2] = put(qq(1, 2), rp.at[2], up_a)
    merge(2, 2)
    relay(2)
    merge(2, 3)
    minus[3] = put(qq(2, 3), rm.at[3], down_a)
    merge(1, 3)
    relay(3)
    products_pair(3)
    products_own(3)
    for c in z_cot:
        arrived(c)
    ut = slots_of(cot_r).T
    up2[...] = jnp.concatenate([ut[:HALF], ut[HALF:]], axis=1)
    for r in range(4):
        merge(3, r)

    def total(r):
        arrived(plus[r])
        arrived(minus[r])
        return q[12 + r].astype(F32) + rp[r].astype(F32) + rm[r].astype(F32)

    (o0, n0), (o1, n1) = CUT
    c0, c1 = pl.ds(o0, n0), pl.ds(o1, n1)
    s[0] = total(0).astype(BF16)
    far_up = put(s.at[0, c0], t2.at[c0], up_b)
    far_dn = put(s.at[0, c1], t2.at[c1], down_b)
    s[1] = total(1).astype(BF16)
    p1 = put(s.at[1, c1], rp2.at[c1], up_b)
    s[2] = total(2).astype(BF16)
    m1 = put(s.at[2, c0], rm2.at[c0], down_b)
    arrived(far_up)
    s[1, c0] = s[1, c0] + t2[c0]
    p2 = put(s.at[1, c0], rp2.at[c0], up_b)
    arrived(far_dn)
    s[2, c1] = s[2, c1] + t2[c1]
    m2 = put(s.at[2, c1], rm2.at[c1], down_b)
    own = total(3)
    for c in (p1, m1, p2, m2):
        arrived(c)

    pre = own + rp2[...].astype(F32) + rm2[...].astype(F32)
    gate = jax.nn.sigmoid(pre)
    slope = gate * (1.0 + pre * (1.0 - gate))
    dbuf[me] = (up2[...] * slope).astype(BF16)

    def hand(da, db):
        i = at(da, db)
        hands[da, db] = put(dbuf.at[i], dbuf.at[i], partner)

    def spread(db):
        i = at(0, db)
        up = put(dbuf.at[i], dbuf.at[i], up_a)
        dn = put(dbuf.at[i], dbuf.at[i], down_a)
        hand(0, db)
        return up, dn

    hands = {}
    b_up = put(dbuf.at[me], dbuf.at[me], up_b)
    b_dn = put(dbuf.at[me], dbuf.at[me], down_b)
    sent = {0: spread(0)}

    ht = (pre * gate).T
    for e in range(8):
        hs[e] = jnp.concatenate(
            [ht[40 * e:40 * e + 40], ht[320 + 40 * e:360 + 40 * e]], axis=0).astype(BF16)
    z_hid = swap(hs, hid_out)
    hid_out[z] = hs[z]

    arrived(b_up)
    i = at(0, 3)
    f_up = put(dbuf.at[i, c0], dbuf.at[i, c0], up_b)
    arrived(b_dn)
    i = at(0, 1)
    f_dn = put(dbuf.at[i, c1], dbuf.at[i, c1], down_b)
    sent[3] = spread(3)
    sent[1] = spread(1)
    fwd = {}

    def arrive(db):
        up, dn = sent[db]
        arrived(up)
        if db in (0, 2):
            i = at(3, db)
            fwd[db] = put(dbuf.at[i], dbuf.at[i], up_a)
        hand(3, db)
        arrived(dn)
        if db in (1, 3):
            i = at(1, db)
            fwd[db] = put(dbuf.at[i], dbuf.at[i], down_a)
        hand(1, db)

    def gradients(dd_of, first=False):
        def flip(r, carry):
            dd = dd_of(r)
            for j in range(7):
                v = dbuf[dd, 16 * j:16 * j + 16].astype(F32)
                dyr[pl.ds(pl.multiple_of(r * HALF + 16 * j, 16), 16)] = (
                    jnp.where(minus_at(dd, j), -v, v).astype(BF16))
            return carry

        lax.fori_loop(0, 4, flip, 0)
        dds = [dd_of(r) for r in range(4)]
        dy = jnp.concatenate([dbuf[dd] for dd in dds], axis=0)
        gmean = dot(jnp.concatenate([wm[dd] for dd in dds], axis=0), dy, TN)
        gpert = dot(jnp.concatenate([wd[dd] for dd in dds], axis=0), dyr[...], TN)
        if first:
            accm[...] = gmean
            accd[...] = gpert
        else:
            accm[...] += gmean
            accd[...] += gpert
        mx[:, 0:256] = dot(dy, ba[...])
        mx[:, 256:512] = dot(dyr[...], bb[...])

        def keep(r, carry):
            dd = dd_of(r)
            rows = pl.ds(pl.multiple_of(r * HALF, 16), HALF)
            for h in range(2):
                gt[2 * dd + h] = mx[rows, h * 128:(h + 1) * 128].astype(BF16)
                gdt[2 * dd + h] = mx[rows, 256 + h * 128:384 + h * 128]
            return carry

        lax.fori_loop(0, 4, keep, 0)

    def gradients_own(da, first=False):
        gradients(lambda r: at(da, r), first)

    def gradients_pair(db):
        for da in range(4):
            arrived(hands[db, da])
        gradients(lambda r: theirs(db, r))

    arrive(0)
    arrived(f_up)
    arrived(f_dn)
    sent[2] = spread(2)
    gradients_own(0, True)
    arrive(3)
    arrive(1)
    gradients_pair(0)
    arrive(2)
    gradients_own(3)
    arrived(fwd[0])
    hand(2, 0)
    gradients_own(1)
    arrived(fwd[3])
    hand(2, 3)
    arrived(fwd[1])
    hand(2, 1)
    gradients_pair(3)
    arrived(fwd[2])
    hand(2, 2)
    gradients_pair(1)
    gradients_own(2)
    gradients_pair(2)

    gp = accm[0:128, 0:320] + accm[128:256, 320:640]
    gn = accd[0:128, 0:320] + accd[128:256, 320:640]
    g = (gp + sgn_t[...] * gn).T
    for e in range(8):
        gs[e] = g[40 * e:40 * e + 40].astype(BF16)
    z_back = swap(gs, back_out)
    back_out[z] = gs[z]

    def store(i, ref, hbm, j):
        cols = pl.ds(pl.multiple_of(i * BLOCK, 128), BLOCK)
        return pltpu.make_async_copy(ref.at[:, cols], hbm.at[:, cols], local.at[2 * i + j])

    def turn(i, carry):
        cols = pl.ds(pl.multiple_of(i * BLOCK, 128), BLOCK)
        rows = pl.ds(8 * i, 8)
        gm[:, cols] = gt[rows].reshape(BLOCK, 128).T
        store(i, gm, gm_hbm, 0).start()
        gr[:, cols] = (gdt[rows].reshape(BLOCK, 128).T * noise[:, cols].astype(F32)
                       * jax.nn.sigmoid(rho[:, cols].astype(F32))).astype(BF16)
        store(i, gr, gr_hbm, 1).start()
        return carry

    lax.fori_loop(0, 8, turn, 0)
    for c in z_hid + z_back:
        arrived(c)

    def settle(i, carry):
        store(i, gm, gm_hbm, 0).wait()
        store(i, gr, gr_hbm, 1).wait()
        return carry

    lax.fori_loop(0, 8, settle, 0)
    for c in copies:
        if id(c) not in done:
            c.wait_recv()
    for c in copies:
        c.wait_send()
    assert len(copies) == COPIES


def layer(rows, words, cot, mean, rho, noise):
    v = pltpu.VMEM
    blk = lambda n: v((n, HALF, 640), BF16)
    one = v((HALF, 640), BF16)
    weight = v((128, UNITS), BF16)
    hbm = pl.BlockSpec(memory_space=pl.ANY)
    return pl.pallas_call(
        layer_kernel,
        in_specs=[VMEM] * 3 + [hbm] * 3,
        out_specs=[VMEM, VMEM, hbm, hbm],
        out_shape=[jax.ShapeDtypeStruct((8, 80, HALF), BF16), jax.ShapeDtypeStruct((8, 40, 128), BF16),
                   jax.ShapeDtypeStruct((128, UNITS), BF16), jax.ShapeDtypeStruct((128, UNITS), BF16)],
        scratch_shapes=[
            weight, weight, weight, v((32, HALF, 256), BF16), v((32, HALF, 256), BF16),
            v((8, 40, 128), BF16), v((8, 40, 128), I32), v((8, 40, 128), I32), v((8, 40, 224), BF16),
            v((2, 128, 640), I32), v((256, 640), BF16), v((256, 640), BF16),
            v((640, 256), BF16), v((640, 256), BF16), v((128, 320), F32), v((HALF, 640), F32),
            v((448, 640), F32), v((448, 640), F32),
            blk(32), blk(16), blk(16), blk(4), blk(4), blk(4), blk(3), one, one, one, blk(32),
            v((8, 80, HALF), BF16), v((448, 640), BF16), v((256, 640), F32), v((256, 640), F32),
            v((64, HALF, 128), BF16), v((64, HALF, 128), F32), v((8, 40, 128), BF16), weight, weight,
            pltpu.SemaphoreType.DMA((COPIES,)), pltpu.SemaphoreType.DMA((COPIES,)),
            pltpu.SemaphoreType.DMA((19,))],
        compiler_params=pltpu.CompilerParams(
            collective_id=1, has_side_effects=True, vmem_limit_bytes=62 * 1024 * 1024),
        name="layer",
    )(rows, words, cot, mean, rho, noise)


def bytes_of(words):
    parts = [(words >> (8 * j)) & 255 for j in range(4)]
    return jnp.concatenate(parts, axis=1).astype(F32).astype(BF16)


def words_of(parts):
    n = parts.shape[1] // 4
    ints = parts.astype(I32)
    return ints[:, :n] | (ints[:, n:2 * n] << 8) | (ints[:, 2 * n:3 * n] << 16) | (ints[:, 3 * n:] << 24)


def on_device(tokens, in_signs, out_signs, expert_ids, route_weight, cotangent,
              mean_weight, rho_weight, noise_weight):
    experts, capacity, slots, topk = 8, 40, 320, 2
    token_count = tokens.shape[0]
    core = lax.rem(lax.axis_index("dp"), 2)

    flat_ids = expert_ids.reshape(-1)
    pairs = token_count * topk
    onehot = (flat_ids[:, None] == jnp.arange(experts, dtype=I32)).astype(BF16)
    lower = (jnp.arange(pairs)[:, None] > jnp.arange(pairs)[None, :]).astype(BF16)
    before = dot(lower, onehot)
    ranks = jnp.sum(before * onehot.astype(F32), axis=1).astype(I32)
    slot_of = (flat_ids * capacity + ranks).reshape(token_count, topk)
    slot_ids = jnp.arange(slots, dtype=I32)
    picks = [slot_of[:, k][:, None] == slot_ids[None, :] for k in range(topk)]
    pick = [p.astype(BF16) for p in picks]
    gather = pick[0] + pick[1]
    slot_weight = sum(
        jnp.sum(jnp.where(p, route_weight[:, k][:, None], 0.0), axis=0) for k, p in enumerate(picks))

    half = lax.dynamic_slice_in_dim(out_signs, core * 112, 112, 1)
    half = jnp.concatenate([half, in_signs, jnp.zeros((token_count, 12), I32)], axis=1)
    send_rows = dot(gather, tokens, TN).astype(BF16)
    send_cot = (dot(gather, cotangent, TN) * slot_weight[:, None]).astype(BF16)
    send_words = words_of(dot(gather, bytes_of(half), TN))
    hid, back, grad_mean, grad_rho = layer(
        *(v.reshape(experts, capacity, -1) for v in (send_rows, send_words, send_cot)),
        mean_weight[0], rho_weight[0], noise_weight[0])
    w0, w1 = route_weight[:, 0:1], route_weight[:, 1:2]
    hidden_out = []
    for h in range(2):
        v = hid[:, 40 * h:40 * h + 40].reshape(slots, -1)
        hidden_out.append(dot(pick[0], v) * w0 + dot(pick[1], v) * w1)
    hidden_out = jnp.concatenate(hidden_out, axis=1).astype(BF16)
    grad_tokens = dot(gather, back.reshape(slots, -1)).astype(BF16)
    return hidden_out, grad_tokens, grad_mean[None], grad_rho[None]


def solution(mesh):
    row = P("expert", "dp")
    full = P("expert", None)
    weight = P("expert", "dp", None)
    return jax.shard_map(
        on_device, mesh=mesh,
        in_specs=(row, row, full, full, full, row, weight, weight, weight),
        out_specs=(row, row, weight, weight), check_vma=False)
```

time: 289 us -> 87.5 us (0.30)
  waiting for transfers between devices: 145 us -> 0 us
  Pallas kernels: 0 us -> 69.9 us
  local copies, waits for them, and re-layouts: 49.7 us -> 7.16 us
  matrix products: 34.9 us -> 6.33 us
  starting transfers between devices: 19.3 us -> 0 us
  blocking collectives: 14.9 us -> 0 us
  between operations: 14.3 us -> 0.75 us
  other arithmetic: 9.89 us -> 3 us
    unnamed x3 -> x0, waiting for transfers between devices: 91.1 us -> none
    pallas_call x0 -> x1, Pallas kernels: none -> 69.9 us  [layer(): pl.pallas_call(layer_kernel, in_specs=[VMEM] * 3 + [hbm] * 3, out_specs=[...]
    all_gather x1 -> x0, waiting for transfers between devices: 39 us -> none  [on_device(): dy = lax.all_gather(dy_local, 'dp', axis=0, tiled=True)]
    dot_general x13 -> x9, matrix products: 34.9 us -> 6.33 us  [dot(): return lax.dot_general(a, b, dims, preferred_element_type=F32)]
    all_to_all x3 -> x0, starting transfers between devices: 19.2 us -> none  [the longest x1 9.01 us: on_device(): lax.all_to_all(send.reshape(experts, capacity, -1), 'expert', 0, 0, tiled...]
    unnamed x24 -> x7, local copies, waits for them, and re-layouts: 24.1 us -> 5.04 us
    shift_right_arithmetic x8 -> x0, local copies, waits for them, and re-layouts: 16.6 us -> none  [the longest x4 16.4 us: on_device(): bit = wt[:, None, :] >> jnp.arange(32, dtype=jnp.int32)[None, :, None] & 1]
    all_to_all x3 -> x0, waiting for transfers between devices: 15.2 us -> none  [the longest x1 7.76 us: on_device(): lax.all_to_all(send.reshape(experts, capacity, -1), 'expert', 0, 0, tiled...]
  transfers between devices with their start and end apart: 5 -> 0, of which waited for: 5 -> 0; matrix products, arithmetic and copies ran while one was open for 5% -> 0% of each run, Pallas kernels for 0% -> 0%
where the time goes in v3:
time: 87.5 us; the launch traced here: 87.1 us
  Pallas kernels  69.9 us (80%)
  local copies, waits for them, and re-layouts  7.16 us (8%)
  matrix products  6.33 us (7%)
  other arithmetic  3 us (3%)
    pallas_call x1, Pallas kernels, layer(): pl.pallas_call(layer_kernel, in_specs=[VMEM] * 3 + [hbm] * 3, out_specs=[...  69.9 us
    dot_general x9, matrix products, dot(): return lax.dot_general(a, b, dims, preferred_element_type=F32)  6.33 us
    unnamed x7, local copies, waits for them, and re-layouts  5.04 us

profile of v3, /device:TPU:1, one launch (start us, length us, event | category | flops | bytes accessed | tf_op | source)
XLA Modules:
  0.0 87.1 jit_solution(2741816132127051300)
XLA Ops:
  0.7 0.1 pad.8.clone
  0.7 0.8 slice_bitcast_fusion
  1.5 0.8 copy.22
  2.3 0.1 eq.45
  2.5 0.2 fusion.5
  2.7 0.1 convert_element_type.42
  2.8 0.1 copy.23
  2.9 0.7 multiply_add_fusion
  3.6 0.2 select_reduce_fusion
  3.8 1.5 %convolution_convert_fusion.1 = bf16[320,128]{1,0:T(8,128)(2,1)} fusion(bf16[128,128]{1,0:T(8,128)(2,1)} %param.9, s32[128]{0:T(128)S(1)} %get-tuple-element.21, s32[128]{0:T(128)S(1)} %get-tuple-element.20), kind=kOutput, calls=%fused_computation.3 | convolution fusion | flops 10854400 | bytes 115712 | tf_op jit(solution)/shard_map/dot_general | solution.py:23
  5.3 1.7 %fusion = bf16[320,224]{1,0:T(8,128)(2,1)} fusion(bf16[128,224]{0,1:T(8,128)(2,1)} %param.14, f32[320]{0:T(512)S(1)} %add.26, s32[128]{0:T(128)S(1)} %get-tuple-element.21, s32[128]{0:T(128)S(1)} %get-tuple-element.20), kind=kOutput, calls=%fused_computation.2 | convolution fusion | flops 18821120 | bytes 203008 | tf_op jit(solution)/shard_map/dot_general | solution.py:23
  7.1 0.8 shift-right-arithmetic_and_fusion.3
  7.8 0.3 convolution_convert_fusion
  8.1 0.7 fusion.7
  8.8 69.9 %layer.1 = (bf16[8,80,112]{2,1,0:T(8,128)(2,1)}, bf16[8,40,128]{2,1,0:T(8,128)(2,1)}, bf16[128,7168]{1,0:T(8,128)(2,1)}, bf16[128,7168]{1,0:T(8,128)(2,1)}) custom-call(bf16[8,40,128]{2,1,0:T(8,128)(2,1)} %bitcast.37, s32[8,40,128]{2,1,0:T(8,128)} %bitcast.35, bf16[8,40,224]{2,1,0:T(8,128)(2,1)} %bitcast.36, bf16[128,7168]{1,0:T(8,128)(2,1)} %bitcast.28, ...), custom_call_target="tpu_custom_call" | custom-call | tf_op jit(solution)/shard_map/layer/pallas_call | solution.py:409
  78.7 1.7 %convolution_convert_fusion.2 = bf16[128,128]{1,0:T(8,128)(2,1)} fusion(bf16[320,128]{1,0:T(8,128)(2,1)} %bitcast.38, s32[128]{0:T(128)S(1)} %get-tuple-element.21, s32[128]{0:T(128)S(1)} %get-tuple-element.20), kind=kOutput, calls=%fused_computation.10 | convolution fusion | flops 10829824 | bytes 115712 | tf_op jit(solution)/shard_map/dot_general | solution.py:23
  80.4 0.9 %fusion.33 = (bf16[8,40,112]{2,1,0:T(8,128)(2,1)S(1)}, bf16[8,40,112]{2,1,0:T(8,128)(2,1)S(1)}) fusion(bf16[8,80,112]{2,1,0:T(8,128)(2,1)} %get-tuple-element.8), kind=kLoop, calls=%fused_computation.59 | loop fusion | bytes 286720 | tf_op jit(solution)/shard_map/slice | solution.py:474
  81.4 0.2 convolution_multiply_fusion.2
  81.6 0.2 fusion.4
  81.8 0.2 convolution_multiply_fusion.4
  82.0 0.2 fusion.3
  82.3 0.6 pad_maximum_fusion
  82.9 3.0 %copy.26 = bf16[1,128,7168]{2,1,0:T(8,128)(2,1)} copy(bf16[1,128,7168]{2,1,0:T(8,128)(2,1)} %bitcast.27) | data formatting | bytes 3670016
  85.9 1.2 %copy.27 = bf16[1,128,7168]{2,1,0:T(8,128)(2,1)} copy(bf16[1,128,7168]{2,1,0:T(8,128)(2,1)S(1)} %bitcast.26) | data formatting | bytes 3670016
  (9 shorter events, 0.1 us)
Async XLA Ops:
  0.6 0.9 %copy-start = (s32[128,224]{0,1:T(8,128)S(1)}, s32[128,224]{0,1:T(8,128)}, u32[]{:S(2)}) copy-start(s32[128,224]{0,1:T(8,128)} %param.11) | copy-start | bytes 344068
  82.9 3.0 %copy-start.1 = (bf16[128,7168]{1,0:T(8,128)(2,1)S(1)}, bf16[128,7168]{1,0:T(8,128)(2,1)}, u32[]{:S(2)}) copy-start(bf16[128,7168]{1,0:T(8,128)(2,1)} %get-tuple-element.11) | copy-start | bytes 5505028

commit v4 on v3

--- a/solution.py
+++ b/solution.py
@@ -19,21 +19,25 @@
 CUT = ((0, 64), (64, 48))
 
 
+NT = (((1,), (1,)), ((), ()))
+
+
 def dot(a, b, dims=NN):
     return lax.dot_general(a, b, dims, preferred_element_type=F32)
 
 
+VLIM = 50
 ZORDER = (4, 3, 5, 2, 6, 1, 7)
 UNITS = 7168
 BLOCK = 896
 COPIES = 35 + 1 + 16 + 12 + 6 + 2 + 2 + 8 + 4 + 16
 
 
-def layer_kernel(rows_in, words_in, cot_in, mean_hbm, rho_hbm, noise_hbm,
-                 hid_out, back_out, gm_hbm, gr_hbm,
-                 mean, rho, noise, wm, wd, rows_r, words_r, words_p, cot_r, w2, bda, bdb, ba, bb, sgn_t,
+def layer_kernel(tokens, in_signs, out_signs, ids, route, cotangent, mean_hbm, rho_hbm, noise_hbm,
+                 hidden_out, grad_tokens, gm, gr,
+                 picks, rows_in, words_in, cot_in, hid_out, back_out, mean, rho, noise, wm, wd, rows_r, words_r, words_p, cot_r, w2, bda, bdb, ba, bb, sgn_t,
                  up2, mx, dx, p, r0, q, t1, rp, rm, s, t2, rp2, rm2, dbuf, hs, dyr, accm, accd,
-                 gt, gdt, gs, gm, gr, send, recv, local):
+                 gt, gdt, gs, send, recv, local):
     me, z = lax.axis_index("dp"), lax.axis_index("expert")
     k = lax.rem(me, 2)
     x, y = me // 8, lax.rem(me // 2, SIDE)
@@ -49,7 +53,7 @@
 
     up_a, down_a, up_b, down_b = at(1, 0), at(3, 0), at(0, 1), at(0, 3)
 
-    loads = [pltpu.make_async_copy(src, dst, local.at[16 + i]) for i, (src, dst) in enumerate(
+    loads = [pltpu.make_async_copy(src, dst, local.at[i]) for i, (src, dst) in enumerate(
         ((rho_hbm, rho), (noise_hbm, noise), (mean_hbm, mean)))]
     for c in loads:
         c.start()
@@ -58,6 +62,30 @@
         pl.semaphore_signal(barrier, inc=1, device_id={"expert": lax.rem(z + o, 8)}, device_id_type=MESH)
     for peer in (up_a, down_a, up_b, down_b, partner):
         pl.semaphore_signal(barrier, inc=1, device_id={"dp": peer}, device_id_type=MESH)
+
+    lane128 = lax.broadcasted_iota(I32, (128, 128), 1)
+    row128 = lax.broadcasted_iota(I32, (128, 128), 0)
+    names = [jnp.broadcast_to(ids[c:c + 1, :], (128, 128)) == row128 for c in range(2)]
+    named = jnp.where(names[0] | names[1], 1.0, 0.0).astype(BF16)
+    before = dot(named, jnp.where(row128 < lane128, 1.0, 0.0).astype(BF16))
+    row320 = lax.broadcasted_iota(I32, (320, 128), 0)
+    hit = []
+    for c in range(2):
+        rank = jnp.sum(jnp.where(names[c], before, 0.0), axis=0, keepdims=True).astype(I32)
+        hit.append(jnp.broadcast_to(ids[c:c + 1, :] * 40 + rank, (320, 128)) == row320)
+        picks[c] = jnp.where(hit[c], 1.0, 0.0).astype(BF16)
+    gather_t = jnp.where(hit[0] | hit[1], 1.0, 0.0).astype(BF16)
+    mine = jnp.where(k == 0, out_signs[0:112, :], out_signs[112:224, :])
+    mine = jnp.concatenate([mine, in_signs[...], jnp.zeros((12, 128), I32)], axis=0)
+    octets = jnp.concatenate(
+        [((mine >> (8 * i)) & 255).astype(F32).astype(BF16) for i in range(4)], axis=0)
+    octets = dot(gather_t, octets, NT).astype(I32)
+    octets = (octets[:, 0:128] | (octets[:, 128:256] << 8)
+              | (octets[:, 256:384] << 16) | (octets[:, 384:512] << 24))
+    sent_rows = dot(gather_t, tokens[...])
+    for e in range(8):
+        words_in[e] = octets[40 * e:40 * e + 40]
+        rows_in[e] = sent_rows[40 * e:40 * e + 40].astype(BF16)
     pl.semaphore_wait(barrier, 12)
 
     copies, done = [], set()
@@ -83,6 +111,10 @@
 
     z_words = swap(words_in, words_r)
     z_rows = swap(rows_in, rows_r)
+    weight_t = jnp.where(hit[0], route[0:1, :], 0.0) + jnp.where(hit[1], route[1:2, :], 0.0)
+    sent_cot = dot(gather_t, cotangent[...], NT) * jnp.sum(weight_t, axis=1, keepdims=True)
+    for e in range(8):
+        cot_in[e] = sent_cot[40 * e:40 * e + 40].astype(BF16)
     z_cot = swap(cot_in, cot_r)
     words_r[z] = words_in[z]
     rows_r[z] = rows_in[z]
@@ -147,16 +179,13 @@
         mx[...] = dot(jnp.concatenate([wm[dd_of(r)] for r in range(4)], axis=0), bda[...])
         dx[...] = dot(jnp.concatenate([wd[dd_of(r)] for r in range(4)], axis=0), bdb[...])
 
-        def combine(r, carry):
+        for r in range(4):
             dd = dd_of(r)
             for j in range(7):
-                rows = pl.ds(pl.multiple_of(r * HALF + 16 * j, 16), 16)
-                pert = dx[rows]
+                o = r * HALF + 16 * j
+                pert = dx[o:o + 16]
                 p[dd, 16 * j:16 * j + 16] = (
-                    mx[rows] + jnp.where(minus_at(dd, j), -pert, pert)).astype(BF16)
-            return carry
-
-        lax.fori_loop(0, 4, combine, 0)
+                    mx[o:o + 16] + jnp.where(minus_at(dd, j), -pert, pert)).astype(BF16)
 
     pair = {}
 
@@ -296,15 +325,12 @@
         hand(1, db)
 
     def gradients(dd_of, first=False):
-        def flip(r, carry):
+        for r in range(4):
             dd = dd_of(r)
             for j in range(7):
+                o = r * HALF + 16 * j
                 v = dbuf[dd, 16 * j:16 * j + 16].astype(F32)
-                dyr[pl.ds(pl.multiple_of(r * HALF + 16 * j, 16), 16)] = (
-                    jnp.where(minus_at(dd, j), -v, v).astype(BF16))
-            return carry
-
-        lax.fori_loop(0, 4, flip, 0)
+                dyr[o:o + 16] = jnp.where(minus_at(dd, j), -v, v).astype(BF16)
         dds = [dd_of(r) for r in range(4)]
         dy = jnp.concatenate([dbuf[dd] for dd in dds], axis=0)
         gmean = dot(jnp.concatenate([wm[dd] for dd in dds], axis=0), dy, TN)
@@ -336,10 +362,10 @@
             arrived(hands[db, da])
         gradients(lambda r: theirs(db, r))
 
-    arrive(0)
     arrived(f_up)
     arrived(f_dn)
     sent[2] = spread(2)
+    arrive(0)
     gradients_own(0, True)
     arrive(3)
     arrive(1)
@@ -368,30 +394,26 @@
     z_back = swap(gs, back_out)
     back_out[z] = gs[z]
 
-    def store(i, ref, hbm, j):
-        cols = pl.ds(pl.multiple_of(i * BLOCK, 128), BLOCK)
-        return pltpu.make_async_copy(ref.at[:, cols], hbm.at[:, cols], local.at[2 * i + j])
-
     def turn(i, carry):
         cols = pl.ds(pl.multiple_of(i * BLOCK, 128), BLOCK)
         rows = pl.ds(8 * i, 8)
         gm[:, cols] = gt[rows].reshape(BLOCK, 128).T
-        store(i, gm, gm_hbm, 0).start()
         gr[:, cols] = (gdt[rows].reshape(BLOCK, 128).T * noise[:, cols].astype(F32)
                        * jax.nn.sigmoid(rho[:, cols].astype(F32))).astype(BF16)
-        store(i, gr, gr_hbm, 1).start()
         return carry
 
     lax.fori_loop(0, 8, turn, 0)
-    for c in z_hid + z_back:
-        arrived(c)
-
-    def settle(i, carry):
-        store(i, gm, gm_hbm, 0).wait()
-        store(i, gr, gr_hbm, 1).wait()
-        return carry
-
-    lax.fori_loop(0, 8, settle, 0)
+    for c in z_hid:
+        arrived(c)
+    for h in range(2):
+        v = jnp.concatenate(
+            [hid_out[e].astype(F32)[40 * h:40 * h + 40] for e in range(8)], axis=0).astype(BF16)
+        hidden_out[HALF * h:HALF * h + HALF] = (
+            dot(v, picks[0], TN) * route[0:1, :] + dot(v, picks[1], TN) * route[1:2, :]).astype(BF16)
+    for c in z_back:
+        arrived(c)
+    grad_tokens[...] = dot(picks[0] + picks[1], slots_of(back_out).astype(BF16), TN).astype(BF16)
+
     for c in copies:
         if id(c) not in done:
             c.wait_recv()
@@ -400,19 +422,21 @@
     assert len(copies) == COPIES
 
 
-def layer(rows, words, cot, mean, rho, noise):
+def layer(*args):
     v = pltpu.VMEM
     blk = lambda n: v((n, HALF, 640), BF16)
     one = v((HALF, 640), BF16)
     weight = v((128, UNITS), BF16)
-    hbm = pl.BlockSpec(memory_space=pl.ANY)
+    hbm = pl.BlockSpec(memory_space=pltpu.HBM)
     return pl.pallas_call(
         layer_kernel,
-        in_specs=[VMEM] * 3 + [hbm] * 3,
-        out_specs=[VMEM, VMEM, hbm, hbm],
-        out_shape=[jax.ShapeDtypeStruct((8, 80, HALF), BF16), jax.ShapeDtypeStruct((8, 40, 128), BF16),
+        in_specs=[VMEM] * 6 + [hbm] * 3,
+        out_specs=[VMEM] * 4,
+        out_shape=[jax.ShapeDtypeStruct((224, 128), BF16), jax.ShapeDtypeStruct((128, 128), BF16),
                    jax.ShapeDtypeStruct((128, UNITS), BF16), jax.ShapeDtypeStruct((128, UNITS), BF16)],
         scratch_shapes=[
+            v((2, 320, 128), BF16), v((8, 40, 128), BF16), v((8, 40, 128), I32), v((8, 40, 224), BF16),
+            v((8, 80, HALF), BF16), v((8, 40, 128), BF16),
             weight, weight, weight, v((32, HALF, 256), BF16), v((32, HALF, 256), BF16),
             v((8, 40, 128), BF16), v((8, 40, 128), I32), v((8, 40, 128), I32), v((8, 40, 224), BF16),
             v((2, 128, 640), I32), v((256, 640), BF16), v((256, 640), BF16),
@@ -420,62 +444,21 @@
             v((448, 640), F32), v((448, 640), F32),
             blk(32), blk(16), blk(16), blk(4), blk(4), blk(4), blk(3), one, one, one, blk(32),
             v((8, 80, HALF), BF16), v((448, 640), BF16), v((256, 640), F32), v((256, 640), F32),
-            v((64, HALF, 128), BF16), v((64, HALF, 128), F32), v((8, 40, 128), BF16), weight, weight,
+            v((64, HALF, 128), BF16), v((64, HALF, 128), F32), v((8, 40, 128), BF16),
             pltpu.SemaphoreType.DMA((COPIES,)), pltpu.SemaphoreType.DMA((COPIES,)),
-            pltpu.SemaphoreType.DMA((19,))],
+            pltpu.SemaphoreType.DMA((3,))],
         compiler_params=pltpu.CompilerParams(
-            collective_id=1, has_side_effects=True, vmem_limit_bytes=62 * 1024 * 1024),
+            collective_id=1, has_side_effects=True, vmem_limit_bytes=VLIM * 1024 * 1024),
         name="layer",
-    )(rows, words, cot, mean, rho, noise)
-
-
-def bytes_of(words):
-    parts = [(words >> (8 * j)) & 255 for j in range(4)]
-    return jnp.concatenate(parts, axis=1).astype(F32).astype(BF16)
-
-
-def words_of(parts):
-    n = parts.shape[1] // 4
-    ints = parts.astype(I32)
-    return ints[:, :n] | (ints[:, n:2 * n] << 8) | (ints[:, 2 * n:3 * n] << 16) | (ints[:, 3 * n:] << 24)
+    )(*args)
 
 
 def on_device(tokens, in_signs, out_signs, expert_ids, route_weight, cotangent,
               mean_weight, rho_weight, noise_weight):
-    experts, capacity, slots, topk = 8, 40, 320, 2
-    token_count = tokens.shape[0]
-    core = lax.rem(lax.axis_index("dp"), 2)
-
-    flat_ids = expert_ids.reshape(-1)
-    pairs = token_count * topk
-    onehot = (flat_ids[:, None] == jnp.arange(experts, dtype=I32)).astype(BF16)
-    lower = (jnp.arange(pairs)[:, None] > jnp.arange(pairs)[None, :]).astype(BF16)
-    before = dot(lower, onehot)
-    ranks = jnp.sum(before * onehot.astype(F32), axis=1).astype(I32)
-    slot_of = (flat_ids * capacity + ranks).reshape(token_count, topk)
-    slot_ids = jnp.arange(slots, dtype=I32)
-    picks = [slot_of[:, k][:, None] == slot_ids[None, :] for k in range(topk)]
-    pick = [p.astype(BF16) for p in picks]
-    gather = pick[0] + pick[1]
-    slot_weight = sum(
-        jnp.sum(jnp.where(p, route_weight[:, k][:, None], 0.0), axis=0) for k, p in enumerate(picks))
-
-    half = lax.dynamic_slice_in_dim(out_signs, core * 112, 112, 1)
-    half = jnp.concatenate([half, in_signs, jnp.zeros((token_count, 12), I32)], axis=1)
-    send_rows = dot(gather, tokens, TN).astype(BF16)
-    send_cot = (dot(gather, cotangent, TN) * slot_weight[:, None]).astype(BF16)
-    send_words = words_of(dot(gather, bytes_of(half), TN))
-    hid, back, grad_mean, grad_rho = layer(
-        *(v.reshape(experts, capacity, -1) for v in (send_rows, send_words, send_cot)),
+    hidden_out, grad_tokens, grad_mean, grad_rho = layer(
+        tokens, in_signs.T, out_signs.T, expert_ids.T, route_weight.T, cotangent.T,
         mean_weight[0], rho_weight[0], noise_weight[0])
-    w0, w1 = route_weight[:, 0:1], route_weight[:, 1:2]
-    hidden_out = []
-    for h in range(2):
-        v = hid[:, 40 * h:40 * h + 40].reshape(slots, -1)
-        hidden_out.append(dot(pick[0], v) * w0 + dot(pick[1], v) * w1)
-    hidden_out = jnp.concatenate(hidden_out, axis=1).astype(BF16)
-    grad_tokens = dot(gather, back.reshape(slots, -1)).astype(BF16)
-    return hidden_out, grad_tokens, grad_mean[None], grad_rho[None]
+    return hidden_out.T, grad_tokens, grad_mean[None], grad_rho[None]
 
 
 def solution(mesh):

time: 87.5 us -> 75.2 us (0.86)
  matrix products: 6.33 us -> 0 us
  Pallas kernels: 69.9 us -> 65.5 us
  other arithmetic: 3 us -> 0 us
  local copies, waits for them, and re-layouts: 7.16 us -> 8.2 us
    dot_general x9 -> x0, matrix products: 6.33 us -> none  [dot(): return lax.dot_general(a, b, dims, preferred_element_type=F32)]
    pallas_call x1, Pallas kernels: 69.9 us -> 65.5 us  [layer(): pl.pallas_call(layer_kernel, in_specs=[VMEM] * 6 + [hbm] * 3, out_specs=[...]
    unnamed x7 -> x16, local copies, waits for them, and re-layouts: 5.04 us -> 8.2 us
    slice x1 -> x0, local copies, waits for them, and re-layouts: 0.94 us -> none  [on_device(): v = hid[:, 40 * h:40 * h + 40].reshape(slots, -1)]
where the time goes in v4:
time: 75.2 us; the launch traced here: 74.3 us
  Pallas kernels  65.5 us (87%)
  local copies, waits for them, and re-layouts  8.2 us (11%)
    pallas_call x1, Pallas kernels, layer(): pl.pallas_call(layer_kernel, in_specs=[VMEM] * 6 + [hbm] * 3, out_specs=[...  65.5 us
    unnamed x16, local copies, waits for them, and re-layouts  8.2 us

profile of v4, /device:TPU:1, one launch (start us, length us, event | category | flops | bytes accessed | tf_op | source)
XLA Modules:
  0.0 74.3 jit_solution(16643073027539840351)
XLA Ops:
  0.6 0.0 copy-start
  0.6 0.9 %copy-done = s32[128,224]{0,1:T(8,128)S(1)} copy-done((s32[128,224]{0,1:T(8,128)S(1)}, s32[128,224]{0,1:T(8,128)}, u32[]{:S(2)}) %copy-start) | copy-done | bytes 114712
  1.5 0.0 copy-start.1
  1.5 0.8 %copy-done.1 = bf16[128,224]{0,1:T(8,128)(2,1)S(1)} copy-done((bf16[128,224]{0,1:T(8,128)(2,1)S(1)}, bf16[128,224]{0,1:T(8,128)(2,1)}, u32[]{:S(2)}) %copy-start.1) | copy-done | bytes 57368
  2.4 0.0 copy-start.2
  2.4 0.8 %copy-done.2 = bf16[128,128]{1,0:T(8,128)(2,1)S(1)} copy-done((bf16[128,128]{1,0:T(8,128)(2,1)S(1)}, bf16[128,128]{1,0:T(8,128)(2,1)}, u32[]{:S(2)}) %copy-start.2) | copy-done | bytes 32792
  3.1 0.0 copy-start.3
  3.1 0.7 copy-done.3
  3.8 0.0 copy-start.4
  3.8 0.7 copy-done.4
  4.5 0.0 copy-start.5
  4.5 0.7 copy-done.5
  5.2 65.5 %layer.1 = (bf16[224,128]{1,0:T(8,128)(2,1)S(1)}, bf16[128,128]{1,0:T(8,128)(2,1)S(1)}, bf16[128,7168]{1,0:T(8,128)(2,1)S(1)}, bf16[128,7168]{1,0:T(8,128)(2,1)S(1)}) custom-call(bf16[128,128]{1,0:T(8,128)(2,1)S(1)} %copy-done.2, s32[4,128]{1,0:T(4,128)S(1)} %bitcast.16, s32[224,128]{1,0:T(8,128)S(1)} %bitcast.13, s32[2,128]{1,0:T(2,128)S(1)} %bitcast.17, ...), custom_call_target="tpu_custom_call" | custom-call | tf_op jit(solution)/shard_map/layer/pallas_call | solution.py:431
  70.6 0.6 copy.17
  71.2 0.6 copy.18
  71.9 1.2 %copy.19 = bf16[1,128,7168]{2,1,0:T(8,128)(2,1)} copy(bf16[1,128,7168]{2,1,0:T(8,128)(2,1)S(1)} %bitcast.12) | data formatting | bytes 3670016
  73.1 1.2 %copy.20 = bf16[1,128,7168]{2,1,0:T(8,128)(2,1)} copy(bf16[1,128,7168]{2,1,0:T(8,128)(2,1)S(1)} %bitcast.11) | data formatting | bytes 3670016
Async XLA Ops:
  0.6 0.9 %copy-start = (s32[128,224]{0,1:T(8,128)S(1)}, s32[128,224]{0,1:T(8,128)}, u32[]{:S(2)}) copy-start(s32[128,224]{0,1:T(8,128)} %param.11) | copy-start | bytes 344068
  1.5 0.8 %copy-start.1 = (bf16[128,224]{0,1:T(8,128)(2,1)S(1)}, bf16[128,224]{0,1:T(8,128)(2,1)}, u32[]{:S(2)}) copy-start(bf16[128,224]{0,1:T(8,128)(2,1)} %param.14) | copy-start | bytes 172036
  2.4 0.8 %copy-start.2 = (bf16[128,128]{1,0:T(8,128)(2,1)S(1)}, bf16[128,128]{1,0:T(8,128)(2,1)}, u32[]{:S(2)}) copy-start(bf16[128,128]{1,0:T(8,128)(2,1)} %tokens.1) | copy-start | bytes 98308
  3.1 0.7 copy-start.3
  3.8 0.7 copy-start.4
  4.5 0.7 copy-start.5

commit v5 on v4

--- a/solution.py
+++ b/solution.py
@@ -30,12 +30,12 @@
 ZORDER = (4, 3, 5, 2, 6, 1, 7)
 UNITS = 7168
 BLOCK = 896
-COPIES = 35 + 1 + 16 + 12 + 6 + 2 + 2 + 8 + 4 + 16
-
-
-def layer_kernel(tokens, in_signs, out_signs, ids, route, cotangent, mean_hbm, rho_hbm, noise_hbm,
+COPIES = 35 + 1 + 16 + 24 + 6 + 2 + 2 + 8 + 8 + 16
+
+
+def layer_kernel(tokens_hbm, ins_hbm, outs_hbm, ids_hbm, route_hbm, cot_hbm, mean_hbm, rho_hbm, noise_hbm,
                  hidden_out, grad_tokens, gm, gr,
-                 picks, rows_in, words_in, cot_in, hid_out, back_out, mean, rho, noise, wm, wd, rows_r, words_r, words_p, cot_r, w2, bda, bdb, ba, bb, sgn_t,
+                 tokens, in_signs, out_signs, ids, route, cotangent, picks, rows_in, words_in, cot_in, hid_out, back_out, mean, rho, noise, wm, wd, rows_r, words_r, words_p, cot_r, w2, bda, bdb, ba, bb, sgn_t,
                  up2, mx, dx, p, r0, q, t1, rp, rm, s, t2, rp2, rm2, dbuf, hs, dyr, accm, accd,
                  gt, gdt, gs, send, recv, local):
     me, z = lax.axis_index("dp"), lax.axis_index("expert")
@@ -54,8 +54,9 @@
     up_a, down_a, up_b, down_b = at(1, 0), at(3, 0), at(0, 1), at(0, 3)
 
     loads = [pltpu.make_async_copy(src, dst, local.at[i]) for i, (src, dst) in enumerate(
-        ((rho_hbm, rho), (noise_hbm, noise), (mean_hbm, mean)))]
-    for c in loads:
+        ((rho_hbm, rho), (noise_hbm, noise), (mean_hbm, mean), (ids_hbm, ids), (outs_hbm, out_signs),
+         (ins_hbm, in_signs), (tokens_hbm, tokens), (route_hbm, route), (cot_hbm, cotangent)))]
+    for c in loads[3:] + loads[:3]:
         c.start()
     barrier = pltpu.get_barrier_semaphore()
     for o in ZORDER:
@@ -63,6 +64,8 @@
     for peer in (up_a, down_a, up_b, down_b, partner):
         pl.semaphore_signal(barrier, inc=1, device_id={"dp": peer}, device_id_type=MESH)
 
+    for c in loads[3:]:
+        c.wait()
     lane128 = lax.broadcasted_iota(I32, (128, 128), 1)
     row128 = lax.broadcasted_iota(I32, (128, 128), 0)
     names = [jnp.broadcast_to(ids[c:c + 1, :], (128, 128)) == row128 for c in range(2)]
@@ -120,7 +123,7 @@
     rows_r[z] = rows_in[z]
     cot_r[z] = cot_in[z]
 
-    for c in loads:
+    for c in loads[:3]:
         c.wait()
 
     def fold(i, carry):
@@ -201,47 +204,36 @@
         arrived(pair[g, r])
         q[4 * g + r] = p[at(OFFS[g], OFFS[r])] + r0[4 * g + r]
 
-    def qq(g, r):
-        return q.at[4 * g + r]
-
     far, plus, minus = {}, {}, {}
+    (o0, n0), (o1, n1) = CUT
+    c0, c1 = pl.ds(o0, n0), pl.ds(o1, n1)
     products_pair(0)
     products_own(0)
     products_pair(1)
     for r in range(4):
         merge(0, r)
-        far[r] = put(qq(0, r), t1.at[r], up_a if r in (0, 3) else down_a)
+        far[r] = (put(q.at[r, c0], t1.at[r, c0], up_a), put(q.at[r, c1], t1.at[r, c1], down_a))
     products_pair(2)
     products_own(1)
     products_own(2)
-
-    def relay(r):
-        arrived(far[r])
-        g = 1 if r in (0, 3) else 2
-        q[4 * g + r] = q[4 * g + r] + t1[r]
-        if g == 1:
-            plus[r] = put(qq(1, r), rp.at[r], up_a)
-        else:
-            minus[r] = put(qq(2, r), rm.at[r], down_a)
-
-    merge(2, 0)
-    minus[0] = put(qq(2, 0), rm.at[0], down_a)
-    merge(1, 0)
-    relay(0)
-    merge(1, 1)
-    plus[1] = put(qq(1, 1), rp.at[1], up_a)
-    merge(2, 1)
-    relay(1)
-    merge(1, 2)
-    plus[2] = put(qq(1, 2), rp.at[2], up_a)
-    merge(2, 2)
-    relay(2)
-    merge(2, 3)
-    minus[3] = put(qq(2, 3), rm.at[3], down_a)
-    merge(1, 3)
-    relay(3)
     products_pair(3)
     products_own(3)
+
+    def relay(r):
+        merge(1, r)
+        plus[r] = [put(q.at[4 + r, c1], rp.at[r, c1], up_a)]
+        merge(2, r)
+        minus[r] = [put(q.at[8 + r, c0], rm.at[r, c0], down_a)]
+        up, dn = far[r]
+        arrived(up)
+        q[4 + r, c0] = q[4 + r, c0] + t1[r, c0]
+        plus[r].append(put(q.at[4 + r, c0], rp.at[r, c0], up_a))
+        arrived(dn)
+        q[8 + r, c1] = q[8 + r, c1] + t1[r, c1]
+        minus[r].append(put(q.at[8 + r, c1], rm.at[r, c1], down_a))
+
+    for r in range(4):
+        relay(r)
     for c in z_cot:
         arrived(c)
     ut = slots_of(cot_r).T
@@ -250,12 +242,10 @@
         merge(3, r)
 
     def total(r):
-        arrived(plus[r])
-        arrived(minus[r])
+        for c in plus[r] + minus[r]:
+            arrived(c)
         return q[12 + r].astype(F32) + rp[r].astype(F32) + rm[r].astype(F32)
 
-    (o0, n0), (o1, n1) = CUT
-    c0, c1 = pl.ds(o0, n0), pl.ds(o1, n1)
     s[0] = total(0).astype(BF16)
     far_up = put(s.at[0, c0], t2.at[c0], up_b)
     far_dn = put(s.at[0, c1], t2.at[c1], down_b)
@@ -314,15 +304,18 @@
     def arrive(db):
         up, dn = sent[db]
         arrived(up)
-        if db in (0, 2):
-            i = at(3, db)
-            fwd[db] = put(dbuf.at[i], dbuf.at[i], up_a)
+        i = at(3, db)
+        fwd[db] = [put(dbuf.at[i, c0], dbuf.at[i, c0], up_a)]
         hand(3, db)
         arrived(dn)
-        if db in (1, 3):
-            i = at(1, db)
-            fwd[db] = put(dbuf.at[i], dbuf.at[i], down_a)
+        i = at(1, db)
+        fwd[db].append(put(dbuf.at[i, c1], dbuf.at[i, c1], down_a))
         hand(1, db)
+
+    def last(db):
+        for c in fwd[db]:
+            arrived(c)
+        hand(2, db)
 
     def gradients(dd_of, first=False):
         for r in range(4):
@@ -372,16 +365,12 @@
     gradients_pair(0)
     arrive(2)
     gradients_own(3)
-    arrived(fwd[0])
-    hand(2, 0)
+    last(0)
     gradients_own(1)
-    arrived(fwd[3])
-    hand(2, 3)
-    arrived(fwd[1])
-    hand(2, 1)
+    last(3)
+    last(1)
     gradients_pair(3)
-    arrived(fwd[2])
-    hand(2, 2)
+    last(2)
     gradients_pair(1)
     gradients_own(2)
     gradients_pair(2)
@@ -430,12 +419,13 @@
     hbm = pl.BlockSpec(memory_space=pltpu.HBM)
     return pl.pallas_call(
         layer_kernel,
-        in_specs=[VMEM] * 6 + [hbm] * 3,
+        in_specs=[hbm] * 9,
         out_specs=[VMEM] * 4,
         out_shape=[jax.ShapeDtypeStruct((224, 128), BF16), jax.ShapeDtypeStruct((128, 128), BF16),
                    jax.ShapeDtypeStruct((128, UNITS), BF16), jax.ShapeDtypeStruct((128, UNITS), BF16)],
         scratch_shapes=[
-            v((2, 320, 128), BF16), v((8, 40, 128), BF16), v((8, 40, 128), I32), v((8, 40, 224), BF16),
+            v((128, 128), BF16), v((4, 128), I32), v((224, 128), I32), v((2, 128), I32), v((2, 128), F32),
+            v((224, 128), BF16), v((2, 320, 128), BF16), v((8, 40, 128), BF16), v((8, 40, 128), I32), v((8, 40, 224), BF16),
             v((8, 80, HALF), BF16), v((8, 40, 128), BF16),
             weight, weight, weight, v((32, HALF, 256), BF16), v((32, HALF, 256), BF16),
             v((8, 40, 128), BF16), v((8, 40, 128), I32), v((8, 40, 128), I32), v((8, 40, 224), BF16),
@@ -446,7 +436,7 @@
             v((8, 80, HALF), BF16), v((448, 640), BF16), v((256, 640), F32), v((256, 640), F32),
             v((64, HALF, 128), BF16), v((64, HALF, 128), F32), v((8, 40, 128), BF16),
             pltpu.SemaphoreType.DMA((COPIES,)), pltpu.SemaphoreType.DMA((COPIES,)),
-            pltpu.SemaphoreType.DMA((3,))],
+            pltpu.SemaphoreType.DMA((9,))],
         compiler_params=pltpu.CompilerParams(
             collective_id=1, has_side_effects=True, vmem_limit_bytes=VLIM * 1024 * 1024),
         name="layer",
@@ -456,7 +446,8 @@
 def on_device(tokens, in_signs, out_signs, expert_ids, route_weight, cotangent,
               mean_weight, rho_weight, noise_weight):
     hidden_out, grad_tokens, grad_mean, grad_rho = layer(
-        tokens, in_signs.T, out_signs.T, expert_ids.T, route_weight.T, cotangent.T,
+        *(pltpu.with_memory_space_constraint(v, pltpu.HBM) for v in (
+            tokens, in_signs.T, out_signs.T, expert_ids.T, route_weight.T, cotangent.T)),
         mean_weight[0], rho_weight[0], noise_weight[0])
     return hidden_out.T, grad_tokens, grad_mean[None], grad_rho[None]
 

time: 75.2 us -> 70.8 us (0.941)
  local copies, waits for them, and re-layouts: 8.2 us -> 3.7 us
    unnamed x16 -> x4, local copies, waits for them, and re-layouts: 8.2 us -> 3.7 us
where the time goes in v5:
time: 70.8 us; the launch traced here: 69.6 us
  Pallas kernels  65.3 us (92%)
  local copies, waits for them, and re-layouts  3.7 us (5%)
    pallas_call x1, Pallas kernels, layer(): pl.pallas_call(layer_kernel, in_specs=[hbm] * 9, out_specs=[VMEM] * 4, ou...  65.3 us
    unnamed x4, local copies, waits for them, and re-layouts  3.7 us

profile of v5, /device:TPU:1, one launch (start us, length us, event | category | flops | bytes accessed | tf_op | source)
XLA Modules:
  0.0 69.6 jit_solution(15845430175023887258)
XLA Ops:
  0.6 65.3 %layer.1 = (bf16[224,128]{1,0:T(8,128)(2,1)S(1)}, bf16[128,128]{1,0:T(8,128)(2,1)S(1)}, bf16[128,7168]{1,0:T(8,128)(2,1)S(1)}, bf16[128,7168]{1,0:T(8,128)(2,1)S(1)}) custom-call(bf16[128,128]{1,0:T(8,128)(2,1)} %tokens_hbm.1, s32[4,128]{1,0:T(4,128)} %bitcast.19, s32[224,128]{1,0:T(8,128)} %bitcast.17, s32[2,128]{1,0:T(2,128)} %bitcast.20, ...), custom_call_target="tpu_custom_call" | custom-call | tf_op jit(solution)/shard_map/layer/pallas_call | solution.py:420
  65.9 0.6 copy.17
  66.6 0.6 copy.18
  67.2 1.2 %copy.19 = bf16[1,128,7168]{2,1,0:T(8,128)(2,1)} copy(bf16[1,128,7168]{2,1,0:T(8,128)(2,1)S(1)} %bitcast.12) | data formatting | bytes 3670016
  68.4 1.2 %copy.20 = bf16[1,128,7168]{2,1,0:T(8,128)(2,1)} copy(bf16[1,128,7168]{2,1,0:T(8,128)(2,1)S(1)} %bitcast.11) | data formatting | bytes 3670016

commit v6 on v5

--- a/solution.py
+++ b/solution.py
@@ -153,18 +153,16 @@
     for w in range(3):
         word = jnp.where(lane // 32 == w, jnp.broadcast_to(words[:, 112 + w:113 + w], (320, 128)), word)
     sgn = (1 - 2 * ((word >> (lane & 31)) & 1)).astype(F32)
+    sgn_t[...] = sgn.T
     for c in z_rows:
         arrived(c)
     plain = slots_of(rows_r)
     signed = plain * sgn
-    sgn_t[...] = sgn.T
-    none_w, none_t = jnp.zeros((128, 320), F32), jnp.zeros((320, 128), F32)
-    for v, wide, tall in ((plain, bda, ba), (signed, bdb, bb)):
+    none_w = jnp.zeros((128, 320), F32)
+    for v, wide in ((plain, bda), (signed, bdb)):
         t = v.T
         wide[0:128] = jnp.concatenate([t, none_w], axis=1).astype(BF16)
         wide[128:256] = jnp.concatenate([none_w, t], axis=1).astype(BF16)
-        tall[0:320] = jnp.concatenate([v, none_t], axis=1).astype(BF16)
-        tall[320:640] = jnp.concatenate([none_t, v], axis=1).astype(BF16)
     arrived(pair_words)
     wt = jnp.concatenate([words_p[e] for e in range(8)], axis=0).T
     w2[1 - k] = jnp.concatenate([wt, wt], axis=1)
@@ -232,6 +230,10 @@
         q[8 + r, c1] = q[8 + r, c1] + t1[r, c1]
         minus[r].append(put(q.at[8 + r, c1], rm.at[r, c1], down_a))
 
+    none_t = jnp.zeros((320, 128), F32)
+    for v, tall in ((slots_of(rows_r), ba), (slots_of(rows_r) * sgn_t[...].T, bb)):
+        tall[0:320] = jnp.concatenate([v, none_t], axis=1).astype(BF16)
+        tall[320:640] = jnp.concatenate([none_t, v], axis=1).astype(BF16)
     for r in range(4):
         relay(r)
     for c in z_cot:
@@ -317,25 +319,32 @@
             arrived(c)
         hand(2, db)
 
-    def gradients(dd_of, first=False):
+    def gradients(dd_of, first=False, keep_for=0):
         for r in range(4):
             dd = dd_of(r)
             for j in range(7):
                 o = r * HALF + 16 * j
                 v = dbuf[dd, 16 * j:16 * j + 16].astype(F32)
-                dyr[o:o + 16] = jnp.where(minus_at(dd, j), -v, v).astype(BF16)
+                dyr[keep_for, o:o + 16] = jnp.where(minus_at(dd, j), -v, v).astype(BF16)
         dds = [dd_of(r) for r in range(4)]
         dy = jnp.concatenate([dbuf[dd] for dd in dds], axis=0)
         gmean = dot(jnp.concatenate([wm[dd] for dd in dds], axis=0), dy, TN)
-        gpert = dot(jnp.concatenate([wd[dd] for dd in dds], axis=0), dyr[...], TN)
+        gpert = dot(jnp.concatenate([wd[dd] for dd in dds], axis=0), dyr[keep_for], TN)
         if first:
             accm[...] = gmean
             accd[...] = gpert
         else:
             accm[...] += gmean
             accd[...] += gpert
+        later = lambda: weights(dd_of, keep_for)
+        if keep_for:
+            return later
+        later()
+
+    def weights(dd_of, kept):
+        dy = jnp.concatenate([dbuf[dd_of(r)] for r in range(4)], axis=0)
         mx[:, 0:256] = dot(dy, ba[...])
-        mx[:, 256:512] = dot(dyr[...], bb[...])
+        mx[:, 256:512] = dot(dyr[kept], bb[...])
 
         def keep(r, carry):
             dd = dd_of(r)
@@ -347,13 +356,13 @@
 
         lax.fori_loop(0, 4, keep, 0)
 
-    def gradients_own(da, first=False):
-        gradients(lambda r: at(da, r), first)
-
-    def gradients_pair(db):
+    def gradients_own(da, first=False, keep_for=0):
+        return gradients(lambda r: at(da, r), first, keep_for)
+
+    def gradients_pair(db, keep_for=0):
         for da in range(4):
             arrived(hands[db, da])
-        gradients(lambda r: theirs(db, r))
+        return gradients(lambda r: theirs(db, r), False, keep_for)
 
     arrived(f_up)
     arrived(f_dn)
@@ -371,9 +380,7 @@
     last(1)
     gradients_pair(3)
     last(2)
-    gradients_pair(1)
-    gradients_own(2)
-    gradients_pair(2)
+    kept = [gradients_pair(1, 1), gradients_own(2, False, 2), gradients_pair(2, 3)]
 
     gp = accm[0:128, 0:320] + accm[128:256, 320:640]
     gn = accd[0:128, 0:320] + accd[128:256, 320:640]
@@ -382,12 +389,14 @@
         gs[e] = g[40 * e:40 * e + 40].astype(BF16)
     z_back = swap(gs, back_out)
     back_out[z] = gs[z]
+    for rest in kept:
+        rest()
 
     def turn(i, carry):
         cols = pl.ds(pl.multiple_of(i * BLOCK, 128), BLOCK)
         rows = pl.ds(8 * i, 8)
-        gm[:, cols] = gt[rows].reshape(BLOCK, 128).T
-        gr[:, cols] = (gdt[rows].reshape(BLOCK, 128).T * noise[:, cols].astype(F32)
+        gm[0, :, cols] = gt[rows].reshape(BLOCK, 128).T
+        gr[0, :, cols] = (gdt[rows].reshape(BLOCK, 128).T * noise[:, cols].astype(F32)
                        * jax.nn.sigmoid(rho[:, cols].astype(F32))).astype(BF16)
         return carry
 
@@ -422,7 +431,7 @@
         in_specs=[hbm] * 9,
         out_specs=[VMEM] * 4,
         out_shape=[jax.ShapeDtypeStruct((224, 128), BF16), jax.ShapeDtypeStruct((128, 128), BF16),
-                   jax.ShapeDtypeStruct((128, UNITS), BF16), jax.ShapeDtypeStruct((128, UNITS), BF16)],
+                   jax.ShapeDtypeStruct((1, 128, UNITS), BF16), jax.ShapeDtypeStruct((1, 128, UNITS), BF16)],
         scratch_shapes=[
             v((128, 128), BF16), v((4, 128), I32), v((224, 128), I32), v((2, 128), I32), v((2, 128), F32),
             v((224, 128), BF16), v((2, 320, 128), BF16), v((8, 40, 128), BF16), v((8, 40, 128), I32), v((8, 40, 224), BF16),
@@ -433,7 +442,7 @@
             v((640, 256), BF16), v((640, 256), BF16), v((128, 320), F32), v((HALF, 640), F32),
             v((448, 640), F32), v((448, 640), F32),
             blk(32), blk(16), blk(16), blk(4), blk(4), blk(4), blk(3), one, one, one, blk(32),
-            v((8, 80, HALF), BF16), v((448, 640), BF16), v((256, 640), F32), v((256, 640), F32),
+            v((8, 80, HALF), BF16), v((4, 448, 640), BF16), v((256, 640), F32), v((256, 640), F32),
             v((64, HALF, 128), BF16), v((64, HALF, 128), F32), v((8, 40, 128), BF16),
             pltpu.SemaphoreType.DMA((COPIES,)), pltpu.SemaphoreType.DMA((COPIES,)),
             pltpu.SemaphoreType.DMA((9,))],
@@ -443,13 +452,37 @@
     )(*args)
 
 
+def out_kernel(hid, tok, gm, gr, hid_hbm, tok_hbm, gm_hbm, gr_hbm, sem):
+    parts = [(hid, hid_hbm), (tok, tok_hbm)]
+    for ref, hbm in ((gm, gm_hbm), (gr, gr_hbm)):
+        parts += [(ref.at[0, pl.ds(32 * i, 32)], hbm.at[0, pl.ds(32 * i, 32)]) for i in range(4)]
+    copies = [pltpu.make_async_copy(src, dst, sem.at[i]) for i, (src, dst) in enumerate(parts)]
+    for c in copies:
+        c.start()
+    for c in copies:
+        c.wait()
+
+
+def out(*arrays):
+    hbm = pl.BlockSpec(memory_space=pl.ANY)
+    return pl.pallas_call(
+        out_kernel,
+        in_specs=[VMEM] * 4,
+        out_specs=[hbm] * 4,
+        out_shape=[jax.ShapeDtypeStruct(v.shape, v.dtype) for v in arrays],
+        scratch_shapes=[pltpu.SemaphoreType.DMA((10,))],
+        compiler_params=pltpu.CompilerParams(vmem_limit_bytes=8 * 1024 * 1024),
+        name="out",
+    )(*arrays)
+
+
 def on_device(tokens, in_signs, out_signs, expert_ids, route_weight, cotangent,
               mean_weight, rho_weight, noise_weight):
-    hidden_out, grad_tokens, grad_mean, grad_rho = layer(
+    hidden_out, grad_tokens, grad_mean, grad_rho = out(*layer(
         *(pltpu.with_memory_space_constraint(v, pltpu.HBM) for v in (
             tokens, in_signs.T, out_signs.T, expert_ids.T, route_weight.T, cotangent.T)),
-        mean_weight[0], rho_weight[0], noise_weight[0])
-    return hidden_out.T, grad_tokens, grad_mean[None], grad_rho[None]
+        mean_weight[0], rho_weight[0], noise_weight[0]))
+    return hidden_out.T, grad_tokens, grad_mean, grad_rho
 
 
 def solution(mesh):

time: 70.8 us -> 67.8 us (0.958)
  local copies, waits for them, and re-layouts: 3.7 us -> 0 us
  Pallas kernels: 65.3 us -> 66.5 us
    unnamed x4 -> x0, local copies, waits for them, and re-layouts: 3.7 us -> none
    pallas_call x0 -> x1, Pallas kernels: none -> 1.94 us  [out(): pl.pallas_call(out_kernel, in_specs=[VMEM] * 4, out_specs=[hbm] * 4, out_...]
    pallas_call x1, Pallas kernels: 65.3 us -> 64.6 us  [layer(): pl.pallas_call(layer_kernel, in_specs=[hbm] * 9, out_specs=[VMEM] * 4, ou...]
where the time goes in v6:
time: 67.8 us; the launch traced here: 67.3 us
  Pallas kernels  66.5 us (98%)
  between operations  0.8 us (1%)
    pallas_call x1, Pallas kernels, layer(): pl.pallas_call(layer_kernel, in_specs=[hbm] * 9, out_specs=[VMEM] * 4, ou...  64.6 us
    pallas_call x1, Pallas kernels, out(): pl.pallas_call(out_kernel, in_specs=[VMEM] * 4, out_specs=[hbm] * 4, out_...  1.94 us

profile of v6, /device:TPU:1, one launch (start us, length us, event | category | flops | bytes accessed | tf_op | source)
XLA Modules:
  0.0 67.3 jit_solution(5124598126934990181)
XLA Ops:
  0.6 64.6 %layer.1 = (bf16[224,128]{1,0:T(8,128)(2,1)S(1)}, bf16[128,128]{1,0:T(8,128)(2,1)S(1)}, bf16[1,128,7168]{2,1,0:T(8,128)(2,1)S(1)}, bf16[1,128,7168]{2,1,0:T(8,128)(2,1)S(1)}) custom-call(bf16[128,128]{1,0:T(8,128)(2,1)} %tokens_hbm.1, s32[4,128]{1,0:T(4,128)} %bitcast.14, s32[224,128]{1,0:T(8,128)} %bitcast.12, s32[2,128]{1,0:T(2,128)} %bitcast.15, ...), custom_call_target="tpu_custom_call" | custom-call | tf_op jit(solution)/shard_map/layer/pallas_call | solution.py:429
  65.2 1.9 %out.1 = (bf16[224,128]{1,0:T(8,128)(2,1)}, bf16[128,128]{1,0:T(8,128)(2,1)}, bf16[1,128,7168]{2,1,0:T(8,128)(2,1)}, bf16[1,128,7168]{2,1,0:T(8,128)(2,1)}) custom-call(bf16[224,128]{1,0:T(8,128)(2,1)S(1)} %get-tuple-element.12.hid, bf16[128,128]{1,0:T(8,128)(2,1)S(1)} %get-tuple-element.13.tok, bf16[1,128,7168]{2,1,0:T(8,128)(2,1)S(1)} %get-tuple-element.14.gm, ...), custom_call_target="tpu_custom_call" | custom-call | tf_op jit(solution)/shard_map/out/pallas_call | solution.py:468

commit v7 on v6

--- a/solution.py
+++ b/solution.py
@@ -208,20 +208,23 @@
     products_pair(0)
     products_own(0)
     products_pair(1)
-    for r in range(4):
+    def start(r):
         merge(0, r)
         far[r] = (put(q.at[r, c0], t1.at[r, c0], up_a), put(q.at[r, c1], t1.at[r, c1], down_a))
+
+    for r in range(3):
+        start(r)
     products_pair(2)
     products_own(1)
     products_own(2)
-    products_pair(3)
-    products_own(3)
-
-    def relay(r):
+
+    def plain_rows(r):
         merge(1, r)
         plus[r] = [put(q.at[4 + r, c1], rp.at[r, c1], up_a)]
         merge(2, r)
         minus[r] = [put(q.at[8 + r, c0], rm.at[r, c0], down_a)]
+
+    def added_rows(r):
         up, dn = far[r]
         arrived(up)
         q[4 + r, c0] = q[4 + r, c0] + t1[r, c0]
@@ -230,12 +233,21 @@
         q[8 + r, c1] = q[8 + r, c1] + t1[r, c1]
         minus[r].append(put(q.at[8 + r, c1], rm.at[r, c1], down_a))
 
+    def relay(r):
+        plain_rows(r)
+        added_rows(r)
+
+    relay(0)
+    products_pair(3)
+    products_own(3)
     none_t = jnp.zeros((320, 128), F32)
     for v, tall in ((slots_of(rows_r), ba), (slots_of(rows_r) * sgn_t[...].T, bb)):
         tall[0:320] = jnp.concatenate([v, none_t], axis=1).astype(BF16)
         tall[320:640] = jnp.concatenate([none_t, v], axis=1).astype(BF16)
-    for r in range(4):
-        relay(r)
+    relay(1)
+    relay(2)
+    start(3)
+    plain_rows(3)
     for c in z_cot:
         arrived(c)
     ut = slots_of(cot_r).T
@@ -261,6 +273,7 @@
     arrived(far_dn)
     s[2, c1] = s[2, c1] + t2[c1]
     m2 = put(s.at[2, c1], rm2.at[c1], down_b)
+    added_rows(3)
     own = total(3)
     for c in (p1, m1, p2, m2):
         arrived(c)

time: 67.8 us -> 71.1 us (1.049)
  Pallas kernels: 66.5 us -> 70.2 us
    pallas_call x1, Pallas kernels: 64.6 us -> 68.3 us  [layer(): pl.pallas_call(layer_kernel, in_specs=[hbm] * 9, out_specs=[VMEM] * 4, ou...]
where the time goes in v7:
time: 71.1 us; the launch traced here: 71 us
  Pallas kernels  70.2 us (99%)
  between operations  0.8 us (1%)
    pallas_call x1, Pallas kernels, layer(): pl.pallas_call(layer_kernel, in_specs=[hbm] * 9, out_specs=[VMEM] * 4, ou...  68.3 us
    pallas_call x1, Pallas kernels, out(): pl.pallas_call(out_kernel, in_specs=[VMEM] * 4, out_specs=[hbm] * 4, out_...  1.94 us

profile of v7, /device:TPU:1, one launch (start us, length us, event | category | flops | bytes accessed | tf_op | source)
XLA Modules:
  0.0 71.0 jit_solution(491279835972915624)
XLA Ops:
  0.6 68.3 %layer.1 = (bf16[224,128]{1,0:T(8,128)(2,1)S(1)}, bf16[128,128]{1,0:T(8,128)(2,1)S(1)}, bf16[1,128,7168]{2,1,0:T(8,128)(2,1)S(1)}, bf16[1,128,7168]{2,1,0:T(8,128)(2,1)S(1)}) custom-call(bf16[128,128]{1,0:T(8,128)(2,1)} %tokens_hbm.1, s32[4,128]{1,0:T(4,128)} %bitcast.14, s32[224,128]{1,0:T(8,128)} %bitcast.12, s32[2,128]{1,0:T(2,128)} %bitcast.15, ...), custom_call_target="tpu_custom_call" | custom-call | tf_op jit(solution)/shard_map/layer/pallas_call | solution.py:442
  68.9 1.9 %out.1 = (bf16[224,128]{1,0:T(8,128)(2,1)}, bf16[128,128]{1,0:T(8,128)(2,1)}, bf16[1,128,7168]{2,1,0:T(8,128)(2,1)}, bf16[1,128,7168]{2,1,0:T(8,128)(2,1)}) custom-call(bf16[224,128]{1,0:T(8,128)(2,1)S(1)} %get-tuple-element.12.hid, bf16[128,128]{1,0:T(8,128)(2,1)S(1)} %get-tuple-element.13.tok, bf16[1,128,7168]{2,1,0:T(8,128)(2,1)S(1)} %get-tuple-element.14.gm, ...), custom_call_target="tpu_custom_call" | custom-call | tf_op jit(solution)/shard_map/out/pallas_call | solution.py:481
